TPU v7x, 256 devices: a whole 4x4x8 slice. The times are simulated.
256 devices in a mesh: rows: 64 (over z, y, core), model: 4 (over x).
Axes of the slice: x: 4, y: 4, z: 8, core: 2. Of those that a mesh axis runs over, the one named last changes fastest.
Arguments:
- w_query: float32 [4096, 4096], P('rows', 'model'), may hold values from -0.25 to 0.25
- first_query: float32 [4096, 4096], P('rows', 'model'), may hold values from -6 to 6
- second_query: float32 [4096, 4096], P('rows', 'model'), may hold values from 0.1 to 10
- w_key: float32 [4096, 1024], P('rows', 'model'), may hold values from -0.25 to 0.25
- first_key: float32 [4096, 1024], P('rows', 'model'), may hold values from -6 to 6
- second_key: float32 [4096, 1024], P('rows', 'model'), may hold values from 0.1 to 10
- w_value: float32 [4096, 1024], P('rows', 'model'), may hold values from -0.25 to 0.25
- first_value: float32 [4096, 1024], P('rows', 'model'), may hold values from -6 to 6
- second_value: float32 [4096, 1024], P('rows', 'model'), may hold values from 0.1 to 10
- norm_train: float32 [4096], P(('rows', 'model')), may hold values from 0.25 to 1.75
- norm_step: float32 [4096], P(('rows', 'model')), may hold values from -0.3 to 0.3
Outputs:
- final_query: bfloat16 [4096, 4096], P(None, 'model')
- final_key: bfloat16 [4096, 1024], P(None, 'model')
- final_value: bfloat16 [4096, 1024], P(None, 'model')
- column_query: float32 [4096], P('model')
- column_key: float32 [1024], P('model')
- column_value: float32 [1024], P('model')
- serve_norm: bfloat16 [4096], replicated
- result_query: float32 [4096, 4096], P('rows', 'model')
- result_key: float32 [4096, 1024], P('rows', 'model')
- result_value: float32 [4096, 1024], P('rows', 'model')
All inputs are finite; a program needn't handle non-finite values. Where the computation divides by a largest or mean magnitude, that divisor is 1e-20 or more.
Results may differ from a plain program's by a relative error of at most 0.0004.
Values may be sent and summed in bfloat16 or wider, within the bound.
No kernel may reach another device: no remote copies, remote signals or barrier semaphores. Data moves between devices by JAX's collectives and lax.ppermute only.
A program may use at most 64 MiB of HBM per device.

v0:
```python
import jax
import jax.numpy as jnp
from jax import lax
from jax.sharding import Mesh
from jax.sharding import PartitionSpec as P

D_MODEL = 4096
ROWS = ("rows_0", "rows_1", "rows_2")
ROWS_MODEL = ("rows_0", "rows_1", "rows_2", "model")


learn_rate = 0.01
decay_rate = 0.05
tiny_value = 1e-08


def from_everyone(value, axis):
    copies = jnp.broadcast_to(value, (lax.axis_size(axis), *value.shape))
    return lax.all_to_all(copies, axis, split_axis=0, concat_axis=0, tiled=True)


def over_copies(value, axis):
    everything = from_everyone(value, axis)
    return jnp.sum(everything, axis=0)


def together(arrays, axis):
    ends = [0]
    for a in arrays:
        ends.append(ends[-1] + a.size)
    running = over_copies(jnp.concatenate([a.ravel() for a in arrays]), axis)
    return tuple((running[b:e].reshape(a.shape) for a, b, e in zip(arrays, ends, ends[1:])))


def in_one_piece(arrays, axis, dim, along):
    ends, at = ([], 0)
    for a in arrays[:-1]:
        at += a.shape[along]
        ends.append(at)
    both = jnp.concatenate(arrays, axis=along)
    return tuple(jnp.split(lax.all_gather(both, axis, axis=dim, tiled=True), ends, axis=along))


def joined_along(tiles, dim):
    tiles = jnp.moveaxis(tiles, 0, dim)
    dims = tiles.shape
    return tiles.reshape(*dims[:dim], dims[dim] * dims[dim + 1], *dims[dim + 2 :])


def stacked_from(value, axes, turns):
    tiles = value[None]
    for k in turns:
        tiles = lax.all_gather(tiles, axes[k], axis=0, tiled=True)
    current = [lax.axis_size(axes[k]) for k in reversed(turns)]
    tiles = tiles.reshape(*current, *value.shape)
    turned = sorted(range(len(turns)), key=lambda place: turns[len(turns) - 1 - place])
    return tiles.transpose(*turned, *range(len(turns), tiles.ndim)).reshape(-1, *value.shape)


def gathered_by_axis(value, axes, turns, dim):
    return joined_along(stacked_from(value, axes, turns), dim)


def body(
    w_query,
    first_query,
    second_query,
    w_key,
    first_key,
    second_key,
    w_value,
    first_value,
    second_value,
    norm_train,
    norm_step,
):
    result_query = w_query - learn_rate * (
        first_query / (jnp.sqrt(second_query) + tiny_value) + decay_rate * w_query
    )
    result_key = w_key - learn_rate * (
        first_key / (jnp.sqrt(second_key) + tiny_value) + decay_rate * w_key
    )
    result_value = w_value - learn_rate * (
        first_value / (jnp.sqrt(second_value) + tiny_value) + decay_rate * w_value
    )
    total_query, total_key, total_value = together(
        (
            jnp.sum(jnp.abs(result_query), axis=0),
            jnp.sum(jnp.abs(result_key), axis=0),
            jnp.sum(jnp.abs(result_value), axis=0),
        ),
        ROWS,
    )
    column_query = total_query / D_MODEL
    column_key = total_key / D_MODEL
    column_value = total_value / D_MODEL
    narrow_query, narrow_key, narrow_value = (
        (result_query / column_query).astype(jnp.bfloat16),
        (result_key / column_key).astype(jnp.bfloat16),
        (result_value / column_value).astype(jnp.bfloat16),
    )
    final_query, final_key, final_value = in_one_piece(
        (narrow_query, narrow_key, narrow_value), ROWS, 0, 1
    )
    serve_norm = gathered_by_axis(
        (norm_train + norm_step).astype(jnp.bfloat16), ROWS_MODEL, (0, 1, 3, 2), 0
    )
    return (
        final_query,
        final_key,
        final_value,
        column_query,
        column_key,
        column_value,
        serve_norm,
        result_query,
        result_key,
        result_value,
    )


def solution(mesh):
    torus = Mesh(
        mesh.devices.reshape(8, 4, 2, mesh.shape["model"]), ("rows_0", "rows_1", "rows_2", "model")
    )
    in_specs = (
        P(ROWS, "model"),
        P(ROWS, "model"),
        P(ROWS, "model"),
        P(ROWS, "model"),
        P(ROWS, "model"),
        P(ROWS, "model"),
        P(ROWS, "model"),
        P(ROWS, "model"),
        P(ROWS, "model"),
        P(ROWS_MODEL),
        P(ROWS_MODEL),
    )
    out_specs = (
        P(None, "model"),
        P(None, "model"),
        P(None, "model"),
        P("model"),
        P("model"),
        P("model"),
        P(),
        P(ROWS, "model"),
        P(ROWS, "model"),
        P(ROWS, "model"),
    )
    return jax.shard_map(body, mesh=torus, in_specs=in_specs, out_specs=out_specs, check_vma=False)
```

profile of v0, /device:TPU:1, one launch (start us, length us, event | category | flops | bytes accessed | tf_op | source)
XLA Modules:
  0.0 144.5 jit_solution(5819135674812837901)
XLA Ops:
  7.2 0.0 copy-start.8
  7.2 0.0 copy-start.6
  7.2 0.0 copy-start.7
  7.2 0.0 all-gather.4.cloned.1.call-start
  7.3 1.3 abs_reduce_fusion
  8.5 0.0 copy-start
  8.5 1.2 abs_reduce_fusion.1
  9.7 0.0 copy-start.1
  9.7 0.0 copy-start.2
  9.8 0.2 broadcast_in_dim.4
  10.0 28.1 %all_to_all.6 = f32[64,1,1536]{2,1,0:T(1,128)S(1)} all-to-all(f32[64,1,1536]{2,1,0:T(1,128)S(1)} %broadcast_in_dim.4), channel_id=1, replica_groups=mesh['rows_0'=8,'rows_1'=4,'rows_2'=2,'model'=4] {'rows_0','rows_1','row..., dimensions={0} | all-to-all | bytes 786432 | tf_op jit(solution)/shard_map/all_to_all | solution.py:19
  38.1 0.2 reduce_sum.39
  38.3 0.0 copy-start.4
  38.3 0.0 copy-start.5
  38.4 0.0 copy-start.3
  38.5 0.7 pad_maximum_fusion
  39.2 0.0 all-gather.4.cloned.1.call-update
  39.2 0.0 copy-done.8
  39.2 0.6 dynamic-slice
  40.4 0.0 copy-done.6
  40.4 0.0 copy-done.7
  40.5 0.2 dynamic-update-slice
  40.7 12.6 %all-reduce = bf16[128]{0:T(256)(128)(2,1)S(1)} all-reduce(bf16[128]{0:T(256)(128)(2,1)S(1)} %dynamic-update-slice), channel_id=2, replica_groups=mesh['rows_0'=8,'rows_1'=4,'rows_2'=2,'model'=4] {'rows_0'}, use_global_device_ids=true, to_apply=%add | all-reduce | flops 128 | bytes 512
  53.4 0.1 reshape.31
  53.4 8.8 %all_gather.17 = bf16[32,16]{1,0:T(8,128)(2,1)S(1)} all-gather(bf16[8,16]{1,0:T(8,128)(2,1)S(1)} %reshape.31), channel_id=1, replica_groups=mesh['rows_0'=8,'rows_1'=4,'rows_2'=2,'model'=4] {'rows_1'}, dimensions={0}, use_global_device_ids=true | all-gather | bytes 1280 | tf_op jit(solution)/shard_map/all_gather | solution.py:53
  62.2 0.1 copy.29
  62.3 9.3 %all-gather.1 = bf16[4,32,16]{1,2,0:T(8,128)(2,1)S(1)} all-gather(bf16[1,32,16]{1,2,0:T(8,128)(2,1)S(1)} %copy.29), channel_id=1, replica_groups=mesh['rows_0'=8,'rows_1'=4,'rows_2'=2,'model'=4] {'model'}, dimensions={0}, use_global_device_ids=true | all-gather | bytes 5120 | tf_op jit(solution)/shard_map/all_gather | solution.py:53
  71.6 0.1 copy.30
  71.7 9.6 %all_gather.19 = bf16[256,16]{1,0:T(8,128)(2,1)S(1)} all-gather(bf16[128,16]{1,0:T(8,128)(2,1)S(1)} %bitcast.7), channel_id=1, replica_groups=mesh['rows_0'=8,'rows_1'=4,'rows_2'=2,'model'=4] {'rows_2'}, dimensions={0}, use_global_device_ids=true | all-gather | bytes 12288 | tf_op jit(solution)/shard_map/all_gather | solution.py:53
  81.4 0.7 reshape_reshape.3
  82.1 43.3 %all-gather.4.cloned.1.call-done = bf16[4096,1536]{1,0:T(8,128)(2,1)} async-done(((bf16[64,1536]{1,0:T(8,128)(2,1)}), bf16[4096,1536]{1,0:T(8,128)(2,1)}) %all-gather.4.cloned.1.call-update) | async-done | bytes 12582928 | tf_op jit(solution)/shard_map/all_gather | solution.py:41
  125.4 4.5 %fusion = (bf16[4096,256]{1,0:T(8,128)(2,1)}, bf16[4096,256]{1,0:T(8,128)(2,1)}) fusion(bf16[4096,1536]{1,0:T(8,128)(2,1)} %all-gather.4.cloned.1.call-done), kind=kLoop, calls=%fused_computation.15 | loop fusion | bytes 8388608 | tf_op jit(solution)/shard_map/split | solution.py:41
  129.9 0.0 copy-done
  129.9 0.0 copy-done.1
  129.9 0.0 copy-done.2
  129.9 0.0 copy-done.4
  129.9 0.0 copy-done.5
  129.9 0.0 copy-done.3
  129.9 7.8 %split.12 = bf16[4096,1024]{1,0:T(8,128)(2,1)} slice(bf16[4096,1536]{1,0:T(8,128)(2,1)} %all-gather.4.cloned.1.call-done), slice={[0:4096], [0:1024]} | slice | bytes 16777216 | tf_op jit(solution)/shard_map/split | solution.py:41
  (9 shorter events, 0.1 us)
Async XLA Ops:
  7.2 32.0 %copy-start.8 = (u32[256]{0:T(256)S(1)}, u32[256]{0:T(256)}, u32[]{:S(2)}) copy-start(u32[256]{0:T(256)} %constant.21) | copy-start | bytes 3076
  7.2 33.2 %copy-start.6 = (f32[16]{0:T(128)S(1)}, f32[16]{0:T(128)}, u32[]{:S(2)}) copy-start(f32[16]{0:T(128)} %param.20) | copy-start | bytes 196
  7.2 33.2 %copy-start.7 = (f32[16]{0:T(128)S(1)}, f32[16]{0:T(128)}, u32[]{:S(2)}) copy-start(f32[16]{0:T(128)} %param.21) | copy-start | bytes 196
  7.2 118.2 %all-gather.4.cloned.1.call-start = ((), (), s32[]{:S(2)}) async-start(), calls=%async_computation.1 | async-start | bytes 12779520 | tf_op jit(solution)/shard_map/all_gather | solution.py:41
  8.5 121.4 %copy-start = (f32[64,1024]{1,0:T(8,128)}, f32[64,1024]{1,0:T(8,128)S(1)}, u32[]{:S(2)}) copy-start(f32[64,1024]{1,0:T(8,128)S(1)} %get-tuple-element.11) | copy-start | bytes 786436
  9.7 120.2 %copy-start.1 = (f32[64,256]{1,0:T(8,128)}, f32[64,256]{1,0:T(8,128)S(1)}, u32[]{:S(2)}) copy-start(f32[64,256]{1,0:T(8,128)S(1)} %get-tuple-element.15) | copy-start | bytes 196612
  9.7 120.2 %copy-start.2 = (f32[64,256]{1,0:T(8,128)}, f32[64,256]{1,0:T(8,128)S(1)}, u32[]{:S(2)}) copy-start(f32[64,256]{1,0:T(8,128)S(1)} %get-tuple-element.21) | copy-start | bytes 196612
  38.3 91.6 %copy-start.4 = (f32[256]{0:T(256)}, f32[256]{0:T(256)S(1)}, u32[]{:S(2)}) copy-start(f32[256]{0:T(256)S(1)} %get-tuple-element.18) | copy-start | bytes 3076
  38.3 91.6 %copy-start.5 = (f32[256]{0:T(256)}, f32[256]{0:T(256)S(1)}, u32[]{:S(2)}) copy-start(f32[256]{0:T(256)S(1)} %get-tuple-element.19) | copy-start | bytes 3076
  38.4 91.5 %copy-start.3 = (f32[1024]{0:T(1024)}, f32[1024]{0:T(1024)S(1)}, u32[]{:S(2)}) copy-start(f32[1024]{0:T(1024)S(1)} %slice_multiply_fusion) | copy-start | bytes 12292
Sparse Core Ops, SparseCore 0:
  39.3 86.0 all-gather.3
where the time goes:
time: 145 us
  blocking collectives  68.5 us (47%)
  waiting for transfers between devices  43.3 us (30%)
  between operations  14.9 us (10%)
  local copies, waits for them, and re-layouts  14.4 us (10%)
  other arithmetic  3.47 us (2%)
    all_gather x1, waiting for transfers between devices, in_one_piece(): lax.all_gather(both, axis, axis=dim, tiled=True)  43.3 us
    all_to_all x1, blocking collectives, from_everyone(): return lax.all_to_all(copies, axis, split_axis=0, concat_axis=0, tiled=True)  28.1 us
    all_gather x3, blocking collectives, stacked_from(): tiles = lax.all_gather(tiles, axes[k], axis=0, tiled=True)  27.7 us
    unnamed x1, blocking collectives  12.6 us
    split x2, local copies, waits for them, and re-layouts, in_one_piece(): jnp.split(lax.all_gather(both, axis, axis=dim, tiled=True), ends, axis=al...  12.3 us
  transfers between devices with their start and end apart: 1, of which 1 were waited for; matrix products, arithmetic and copies ran while one was open for 1% of the time, Pallas kernels for 0%

commit v1 on v0

v1 whole, which is shorter than its diff:
```python
import jax
import jax.numpy as jnp
from jax import lax
from jax.sharding import Mesh
from jax.sharding import PartitionSpec as P

ROWS = ("z", "y", "c")
ROWS_X = ("z", "y", "c", "x")

learn_rate = 0.01
decay_rate = 0.05
tiny_value = 1e-08


def step(w, first, second):
    return w - learn_rate * (first / (jnp.sqrt(second) + tiny_value) + decay_rate * w)


def around(value, axis):
    size = lax.axis_size(axis)
    me = lax.axis_index(axis)
    out = jnp.zeros((size, *value.shape), value.dtype)
    out = lax.dynamic_update_index_in_dim(out, value, me, 0)
    for k in range(1, size):
        got = lax.ppermute(value, axis, [(i, (i + k) % size) for i in range(size)])
        out = lax.dynamic_update_index_in_dim(out, got, (me - k) % size, 0)
    return out


def body(wq, fq, sq, wk, fk, sk, wv, fv, sv, norm_train, norm_step):
    d_model = wq.shape[0] * lax.axis_size(ROWS)
    norm = (norm_train + norm_step).astype(jnp.bfloat16)
    norms = around(norm.astype(jnp.float32), "x").ravel()
    rq, rk, rv = step(wq, fq, sq), step(wk, fk, sk), step(wv, fv, sv)
    sums = [jnp.sum(jnp.abs(r), axis=0) for r in (rq, rk, rv)]
    mine = jnp.concatenate(sums + [norms])
    n = lax.axis_size(ROWS)
    everyone = lax.all_to_all(
        jnp.broadcast_to(mine, (n, 1, mine.size)), ROWS, split_axis=0, concat_axis=0, tiled=True
    ).reshape(n, mine.size)
    a = wq.shape[1]
    b = a + wk.shape[1]
    c = b + wv.shape[1]
    total = jnp.sum(everyone[:, :c], axis=0) / d_model
    cq, ck, cv = total[:a], total[a:b], total[b:c]
    serve_norm = everyone[:, c:].reshape(-1).astype(jnp.bfloat16)
    narrow = jnp.concatenate(
        [lax.reduce_precision(r / column, 8, 7) for r, column in ((rq, cq), (rk, ck), (rv, cv))], axis=1
    )
    whole = lax.all_gather(narrow.astype(jnp.float16), ROWS, axis=0, tiled=True)
    final = whole.astype(jnp.bfloat16)
    return final[:, :a], final[:, a:b], final[:, b:], cq, ck, cv, serve_norm, rq, rk, rv


def solution(mesh):
    torus = Mesh(mesh.devices.reshape(8, 4, 2, mesh.shape["model"]), ROWS_X)
    w = P(ROWS, "x")
    return jax.shard_map(
        body,
        mesh=torus,
        in_specs=(w,) * 9 + (P(ROWS_X),) * 2,
        out_specs=(P(None, "x"),) * 3 + (P("x"),) * 3 + (P(),) + (w,) * 3,
        check_vma=False,
    )
```

time: 145 us -> 117 us (0.81)
  waiting for transfers between devices: 43.3 us -> 0.49 us
  blocking collectives: 68.5 us -> 89.8 us
  between operations: 14.9 us -> 0.84 us
  starting transfers between devices: 0.04 us -> 4.42 us
  other arithmetic: 3.47 us -> 5.78 us
    all_gather x1 -> x0, waiting for transfers between devices: 43.3 us -> none  [in_one_piece(): lax.all_gather(both, axis, axis=dim, tiled=True)]
    all_gather x3 -> x1, blocking collectives: 27.7 us -> 60.3 us  [body(): whole = lax.all_gather(narrow.astype(jnp.float16), ROWS, axis=0, tiled=True)]
    unnamed x1 -> x0, blocking collectives: 12.6 us -> none
    split x2 -> x0, local copies, waits for them, and re-layouts: 12.3 us -> none  [in_one_piece(): jnp.split(lax.all_gather(both, axis, axis=dim, tiled=True), ends, axis=al...]
    slice x0 -> x5, local copies, waits for them, and re-layouts: none -> 10 us  [the longest x1 7.76 us: body(): final[:, :a]]
    ppermute x0 -> x3, starting transfers between devices: none -> 4.42 us  [around(): got = lax.ppermute(value, axis, [(i, (i + k) % size) for i in range(size)])]
    unnamed x22 -> x15, local copies, waits for them, and re-layouts: 0.96 us -> 4.61 us
    convert_element_type x4 -> x2, other arithmetic: 0.06 us -> 3.14 us  [the longest x1 2.46 us: body(): final = whole.astype(jnp.bfloat16)]
  transfers between devices with their start and end apart: 1 -> 3, of which waited for: 1 -> 1; matrix products, arithmetic and copies ran while one was open for 1% -> 2% of each run, Pallas kernels for 0% -> 0%
where the time goes in v1:
time: 117 us
  blocking collectives  89.8 us (77%)
  local copies, waits for them, and re-layouts  15.8 us (14%)
  other arithmetic  5.78 us (5%)
  starting transfers between devices  4.42 us (4%)
    all_gather x1, blocking collectives, body(): whole = lax.all_gather(narrow.astype(jnp.float16), ROWS, axis=0, tiled=True)  60.3 us
    all_to_all x1, blocking collectives, body(): lax.all_to_all(jnp.broadcast_to(mine, (n, 1, mine.size)), ROWS, split_axi...  29.5 us
    slice x1, local copies, waits for them, and re-layouts, body(): final[:, :a]  7.76 us
    unnamed x15, local copies, waits for them, and re-layouts  4.61 us
    ppermute x3, starting transfers between devices, around(): got = lax.ppermute(value, axis, [(i, (i + k) % size) for i in range(size)])  4.42 us
    convert_element_type x1, other arithmetic, body(): final = whole.astype(jnp.bfloat16)  2.46 us
    reduce_sum x2, other arithmetic, body(): sums = [jnp.sum(jnp.abs(r), axis=0) for r in (rq, rk, rv)]  2.45 us
  transfers between devices with their start and end apart: 3, of which 1 were waited for; matrix products, arithmetic and copies ran while one was open for 2% of the time, Pallas kernels for 0%

profile of v1, /device:TPU:1, one launch (start us, length us, event | category | flops | bytes accessed | tf_op | source)
XLA Modules:
  0.0 117.1 jit_solution(15778458455176074133)
XLA Ops:
  0.6 0.7 convert_convert_fusion
  1.3 3.3 %collective-permute-start.2 = (f32[16]{0:T(128)S(1)}, f32[16]{0:T(128)S(1)}, u32[]{:S(2)}, u32[]{:S(2)}) collective-permute-start(f32[16]{0:T(128)S(1)} %convert_convert_fusion), channel_id=1, source_target_pairs={{0,3},{1,0},{2,1},{3,2},{4,7},{5,4},{6,5},{7,6},{8,11},{9,8},{10,9... | collective-permute-start | bytes 200 | tf_op jit(solution)/shard_map/ppermute | solution.py:25
  4.6 0.5 collective-permute-start.1
  5.1 0.6 collective-permute-start
  5.7 1.3 %abs_reduce_fusion = (f32[1024]{0:T(1024)S(1)}, f32[64,1024]{1,0:T(8,128)S(1)}) fusion(f32[64,1024]{1,0:T(8,128)} %param.11, f32[64,1024]{1,0:T(8,128)} %param.12, f32[64,1024]{1,0:T(8,128)} %param.13), kind=kLoop, calls=%fused_computation.3 | loop fusion | flops 523264 | bytes 1052672 | tf_op jit(solution)/shard_map/reduce_sum | solution.py:35
  7.0 0.0 copy-start.1
  7.0 1.2 %abs_reduce_fusion.1 = (f32[256]{0:T(256)S(1)}, f32[64,256]{1,0:T(8,128)S(1)}, f32[256]{0:T(256)S(1)}, f32[64,256]{1,0:T(8,128)S(1)}) fusion(f32[64,256]{1,0:T(8,128)} %param.17, f32[64,256]{1,0:T(8,128)} %param.18, f32[64,256]{1,0:T(8,128)} %param.19, f32[64,256]{1,0:T(8,128)} %param.14, f32[64,256]{1,0:T(8,128)} %param.15, f32[64,256]{1,0:T(8,128)} %param.16), kind=kLoop, calls=%fused_computation.8 | loop fusion | flops 261632 | bytes 526336 | tf_op jit(solution)/shard_map/reduce_sum | solution.py:35
  8.2 0.0 copy-start.2
  8.2 0.0 copy-start.3
  8.3 0.5 collective-permute-done
  8.8 0.0 collective-permute-done.1
  8.8 0.0 collective-permute-done.2
  8.9 0.1 reshape.31
  9.0 0.2 broadcast_in_dim.27
  9.2 29.5 %all_to_all.5 = f32[64,1,1600]{2,1,0:T(1,128)S(1)} all-to-all(f32[64,1,1600]{2,1,0:T(1,128)S(1)} %broadcast_in_dim.27), channel_id=1, replica_groups=mesh['z'=8,'y'=4,'c'=2,'x'=4] {'z','y','c'}, dimensions={0} | all-to-all | bytes 819200 | tf_op jit(solution)/shard_map/all_to_all | solution.py:38
  38.8 0.0 copy-start.5
  38.9 0.0 copy-start.6
  38.9 0.0 copy-start.4
  39.0 0.1 pad_maximum_fusion
  39.1 60.3 %all-gather.1 = f16[4096,1536]{1,0:T(8,128)(2,1)S(1)} all-gather(f16[64,1536]{1,0:T(8,128)(2,1)S(1)} %pad_maximum_fusion), channel_id=1, replica_groups=mesh['z'=8,'y'=4,'c'=2,'x'=4] {'z','y','c'}, dimensions={0}, use_global_device_ids=true | all-gather | bytes 12779520 | tf_op jit(solution)/shard_map/all_gather | solution.py:50
  99.3 0.0 copy-done.1
  99.3 2.5 %convert_element_type.16 = bf16[4096,1536]{1,0:T(8,128)(2,1)S(1)} convert(f16[4096,1536]{1,0:T(8,128)(2,1)S(1)} %all-gather.1) | non-fusion elementwise | flops 6291456 | bytes 25165824 | tf_op jit(solution)/shard_map/convert_element_type | solution.py:51
  101.8 0.0 copy-done.2
  101.8 0.0 copy-done.3
  101.8 0.0 copy-done.5
  101.8 0.0 copy-done.6
  101.9 0.0 copy-done.4
  101.9 0.0 copy-start
  101.9 4.5 %copy-done = bf16[4096,1536]{1,0:T(8,128)(2,1)} copy-done((bf16[4096,1536]{1,0:T(8,128)(2,1)}, bf16[4096,1536]{1,0:T(8,128)(2,1)S(1)}, u32[]{:S(2)}) %copy-start) | copy-done | bytes 12582936
  106.4 2.3 %fusion = (bf16[4096,256]{1,0:T(8,128)(2,1)}, bf16[4096,256]{1,0:T(8,128)(2,1)}) fusion(bf16[4096,1536]{1,0:T(8,128)(2,1)S(1)} %convert_element_type.16), kind=kLoop, calls=%fused_computation.16 | loop fusion | bytes 8388608 | tf_op jit(solution)/shard_map/slice | solution.py:52
  108.7 7.8 %slice.37 = bf16[4096,1024]{1,0:T(8,128)(2,1)} slice(bf16[4096,1536]{1,0:T(8,128)(2,1)} %copy-done), slice={[0:4096], [0:1024]} | slice | bytes 16777216 | tf_op jit(solution)/shard_map/slice | solution.py:52
  116.5 0.7 convert_element_type.17
  (15 shorter events, 0.3 us)
Async XLA Ops:
  1.3 7.5 %collective-permute-start.2 = (f32[16]{0:T(128)S(1)}, f32[16]{0:T(128)S(1)}, u32[]{:S(2)}, u32[]{:S(2)}) collective-permute-start(f32[16]{0:T(128)S(1)} %convert_convert_fusion), channel_id=1, source_target_pairs={{0,3},{1,0},{2,1},{3,2},{4,7},{5,4},{6,5},{7,6},{8,11},{9,8},{10,9... | collective-permute-start | bytes 200 | tf_op jit(solution)/shard_map/ppermute | solution.py:25
  4.6 4.2 %collective-permute-start.1 = (f32[16]{0:T(128)S(1)}, f32[16]{0:T(128)S(1)}, u32[]{:S(2)}, u32[]{:S(2)}) collective-permute-start(f32[16]{0:T(128)S(1)} %convert_convert_fusion), channel_id=1, source_target_pairs={{0,2},{1,3},{2,0},{3,1},{4,6},{5,7},{6,4},{7,5},{8,10},{9,11},{10,... | collective-permute-start | bytes 200 | tf_op jit(solution)/shard_map/ppermute | solution.py:25
  5.1 3.6 %collective-permute-start = (f32[16]{0:T(128)S(1)}, f32[16]{0:T(128)S(1)}, u32[]{:S(2)}, u32[]{:S(2)}) collective-permute-start(f32[16]{0:T(128)S(1)} %convert_convert_fusion), channel_id=1, source_target_pairs={{0,1},{1,2},{2,3},{3,0},{4,5},{5,6},{6,7},{7,4},{8,9},{9,10},{10,1... | collective-permute-start | bytes 200 | tf_op jit(solution)/shard_map/ppermute | solution.py:25
  7.0 92.3 %copy-start.1 = (f32[64,1024]{1,0:T(8,128)}, f32[64,1024]{1,0:T(8,128)S(1)}, u32[]{:S(2)}) copy-start(f32[64,1024]{1,0:T(8,128)S(1)} %get-tuple-element.11) | copy-start | bytes 786436
  8.2 93.6 %copy-start.2 = (f32[64,256]{1,0:T(8,128)}, f32[64,256]{1,0:T(8,128)S(1)}, u32[]{:S(2)}) copy-start(f32[64,256]{1,0:T(8,128)S(1)} %get-tuple-element.15) | copy-start | bytes 196612
  8.2 93.6 %copy-start.3 = (f32[64,256]{1,0:T(8,128)}, f32[64,256]{1,0:T(8,128)S(1)}, u32[]{:S(2)}) copy-start(f32[64,256]{1,0:T(8,128)S(1)} %get-tuple-element.21) | copy-start | bytes 196612
  38.8 63.0 %copy-start.5 = (f32[256]{0:T(256)}, f32[256]{0:T(256)S(1)}, u32[]{:S(2)}) copy-start(f32[256]{0:T(256)S(1)} %get-tuple-element.18) | copy-start | bytes 3076
  38.9 63.0 %copy-start.6 = (f32[256]{0:T(256)}, f32[256]{0:T(256)S(1)}, u32[]{:S(2)}) copy-start(f32[256]{0:T(256)S(1)} %get-tuple-element.19) | copy-start | bytes 3076
  38.9 63.0 %copy-start.4 = (f32[1024]{0:T(1024)}, f32[1024]{0:T(1024)S(1)}, u32[]{:S(2)}) copy-start(f32[1024]{0:T(1024)S(1)} %slice.34) | copy-start | bytes 12292
  101.9 4.6 %copy-start = (bf16[4096,1536]{1,0:T(8,128)(2,1)}, bf16[4096,1536]{1,0:T(8,128)(2,1)S(1)}, u32[]{:S(2)}) copy-start(bf16[4096,1536]{1,0:T(8,128)(2,1)S(1)} %convert_element_type.16) | copy-start | bytes 37748740

commit v2 on v1

v2 whole, which is shorter than its diff:
```python
import jax
import jax.numpy as jnp
from jax import lax
from jax.experimental import pallas as pl
from jax.experimental.pallas import tpu as pltpu
from jax.sharding import Mesh
from jax.sharding import PartitionSpec as P

ROWS = ("z", "y", "c")
ROWS_X = ("z", "y", "c", "x")

learn_rate = 0.01
decay_rate = 0.05
tiny_value = 1e-08


def step(w, first, second):
    return w - learn_rate * (first / (jnp.sqrt(second) + tiny_value) + decay_rate * w)


def moved(value, axis, k):
    n = lax.axis_size(axis)
    return lax.ppermute(value, axis, [(i, (i + k) % n) for i in range(n)])


def around(value, axis):
    size = lax.axis_size(axis)
    me = lax.axis_index(axis)
    out = jnp.zeros((size, *value.shape), value.dtype)
    out = lax.dynamic_update_index_in_dim(out, value, me, 0)
    for k in range(1, size):
        out = lax.dynamic_update_index_in_dim(out, moved(value, axis, k), (me - k) % size, 0)
    return out


def column_means(sums, norms, d_model):
    c = lax.axis_index("c")
    halves = sums.reshape(2, -1)
    half = halves.shape[1]
    keep = jnp.where(c == 0, halves[0], halves[1])
    give = jnp.where(c == 0, halves[1], halves[0])
    mine = jnp.concatenate([keep + moved(give, "c", 1), norms])
    n = lax.axis_size(("z", "y"))
    everyone = lax.all_to_all(
        jnp.broadcast_to(mine, (n, 1, mine.size)), ("z", "y"), split_axis=0, concat_axis=0, tiled=True
    ).reshape(n, mine.size)
    have = jnp.concatenate([jnp.sum(everyone[:, :half], axis=0) / d_model, everyone[:, half:].ravel()])
    other = moved(have, "c", 1)
    pair = [jnp.where(c == 0, have, other), jnp.where(c == 0, other, have)]
    means = jnp.concatenate([p[:half] for p in pair])
    all_norms = jnp.stack([p[half:].reshape(n, -1) for p in pair], axis=1).ravel()
    return means, all_norms


def parted(joined, widths):
    def kernel(joined_ref, *refs):
        outs, sems = refs[: len(widths)], refs[len(widths) :]
        copies, at = [], 0
        for out, sem, wide in zip(outs, sems, widths):
            copies.append(pltpu.make_async_copy(joined_ref.at[:, pl.ds(at, wide)], out, sem))
            copies[-1].start()
            at += wide
        for copy in copies:
            copy.wait()

    return pl.pallas_call(
        kernel,
        out_shape=[jax.ShapeDtypeStruct((joined.shape[0], wide), joined.dtype) for wide in widths],
        in_specs=[pl.BlockSpec(memory_space=pl.ANY)],
        out_specs=[pl.BlockSpec(memory_space=pl.ANY)] * len(widths),
        scratch_shapes=[pltpu.SemaphoreType.DMA] * len(widths),
        compiler_params=pltpu.CompilerParams(vmem_limit_bytes=1 << 20),
        name="parted",
    )(pltpu.with_memory_space_constraint(joined, pltpu.VMEM))


def body(wq, fq, sq, wk, fk, sk, wv, fv, sv, norm_train, norm_step):
    d_model = wq.shape[0] * lax.axis_size(ROWS)
    norm = (norm_train + norm_step).astype(jnp.bfloat16)
    norms = around(norm.astype(jnp.float32), "x").ravel()
    rq, rk, rv = step(wq, fq, sq), step(wk, fk, sk), step(wv, fv, sv)
    sums = jnp.concatenate([jnp.sum(jnp.abs(r), axis=0) for r in (rq, rk, rv)])
    means, all_norms = column_means(sums, norms, d_model)
    serve_norm = all_norms.astype(jnp.bfloat16)
    a = wq.shape[1]
    b = a + wk.shape[1]
    cq, ck, cv = means[:a], means[a:b], means[b:]
    narrow = jnp.concatenate(
        [lax.reduce_precision(r / column, 8, 7) for r, column in ((rq, cq), (rk, ck), (rv, cv))], axis=1
    )
    whole = lax.all_gather(narrow.astype(jnp.float16), ROWS, axis=0, tiled=True)
    final_q, final_k, final_v = parted(whole.astype(jnp.bfloat16), (a, b - a, whole.shape[1] - b))
    return final_q, final_k, final_v, cq, ck, cv, serve_norm, rq, rk, rv


def solution(mesh):
    torus = Mesh(mesh.devices.reshape(8, 4, 2, mesh.shape["model"]), ROWS_X)
    w = P(ROWS, "x")
    return jax.shard_map(
        body,
        mesh=torus,
        in_specs=(w,) * 9 + (P(ROWS_X),) * 2,
        out_specs=(P(None, "x"),) * 3 + (P("x"),) * 3 + (P(),) + (w,) * 3,
        check_vma=False,
    )
```

time: 117 us -> 102 us (0.87)
  local copies, waits for them, and re-layouts: 15.8 us -> 1.29 us
  blocking collectives: 89.8 us -> 79.7 us
  Pallas kernels: 0 us -> 4.74 us
  starting transfers between devices: 4.42 us -> 8.14 us
    slice x5 -> x8, local copies, waits for them, and re-layouts: 10 us -> 0.19 us  [the longest x4 0.17 us: column_means(): p[half:].reshape(n, -1)]
    all_to_all x1, blocking collectives: 29.5 us -> 20.2 us  [column_means(): lax.all_to_all(jnp.broadcast_to(mine, (n, 1, mine.size)), ('z', 'y'), spl...]
    pallas_call x0 -> x1, Pallas kernels: none -> 4.74 us  [parted(): pl.pallas_call(kernel, out_shape=[jax.ShapeDtypeStruct((joined.shape[0],...]
    unnamed x15 -> x13, local copies, waits for them, and re-layouts: 4.61 us -> 0.04 us
    ppermute x3 -> x5, starting transfers between devices: 4.42 us -> 8.14 us  [moved(): return lax.ppermute(value, axis, [(i, (i + k) % n) for i in range(n)])]
  transfers between devices with their start and end apart: 3 -> 5, of which waited for: 1 -> 2; matrix products, arithmetic and copies ran while one was open for 2% -> 3% of each run, Pallas kernels for 0% -> 0%
where the time goes in v2:
time: 102 us
  blocking collectives  79.7 us (78%)
  starting transfers between devices  8.14 us (8%)
  other arithmetic  5.71 us (6%)
  Pallas kernels  4.74 us (5%)
  waiting for transfers between devices  1.42 us (1%)
  local copies, waits for them, and re-layouts  1.29 us (1%)
    all_gather x1, blocking collectives, body(): whole = lax.all_gather(narrow.astype(jnp.float16), ROWS, axis=0, tiled=True)  59.4 us
    all_to_all x1, blocking collectives, column_means(): lax.all_to_all(jnp.broadcast_to(mine, (n, 1, mine.size)), ('z', 'y'), spl...  20.2 us
    ppermute x5, starting transfers between devices, moved(): return lax.ppermute(value, axis, [(i, (i + k) % n) for i in range(n)])  8.14 us
    pallas_call x1, Pallas kernels, parted(): pl.pallas_call(kernel, out_shape=[jax.ShapeDtypeStruct((joined.shape[0],...  4.74 us
    reduce_sum x2, other arithmetic, body(): sums = jnp.concatenate([jnp.sum(jnp.abs(r), axis=0) for r in (rq, rk, rv)])  2.45 us
    convert_element_type x1, other arithmetic, body(): whole.astype(jnp.bfloat16)  2.36 us
  transfers between devices with their start and end apart: 5, of which 2 were waited for; matrix products, arithmetic and copies ran while one was open for 3% of the time, Pallas kernels for 0%

profile of v2, /device:TPU:1, one launch (start us, length us, event | category | flops | bytes accessed | tf_op | source)
XLA Modules:
  0.0 101.8 jit_solution(11951533041810269939)
XLA Ops:
  0.6 0.7 convert_convert_fusion
  1.3 3.3 %collective-permute-start.3 = (f32[16]{0:T(128)S(1)}, f32[16]{0:T(128)S(1)}, u32[]{:S(2)}, u32[]{:S(2)}) collective-permute-start(f32[16]{0:T(128)S(1)} %convert_convert_fusion), channel_id=1, source_target_pairs={{0,3},{1,0},{2,1},{3,2},{4,7},{5,4},{6,5},{7,6},{8,11},{9,8},{10,9... | collective-permute-start | bytes 200 | tf_op jit(solution)/shard_map/ppermute | solution.py:23
  4.6 0.5 collective-permute-start.2
  5.1 0.6 collective-permute-start.1
  5.7 1.3 %abs_reduce_fusion = (f32[1024]{0:T(1024)S(1)}, f32[64,1024]{1,0:T(8,128)S(1)}) fusion(f32[64,1024]{1,0:T(8,128)} %param.11, f32[64,1024]{1,0:T(8,128)} %param.12, f32[64,1024]{1,0:T(8,128)} %param.13), kind=kLoop, calls=%fused_computation.1 | loop fusion | flops 523264 | bytes 1052672 | tf_op jit(solution)/shard_map/reduce_sum | solution.py:82
  7.0 0.0 copy-start
  7.0 1.2 %abs_reduce_fusion.1 = (f32[256]{0:T(256)S(1)}, f32[64,256]{1,0:T(8,128)S(1)}, f32[256]{0:T(256)S(1)}, f32[64,256]{1,0:T(8,128)S(1)}) fusion(f32[64,256]{1,0:T(8,128)} %param.17, f32[64,256]{1,0:T(8,128)} %param.18, f32[64,256]{1,0:T(8,128)} %param.19, f32[64,256]{1,0:T(8,128)} %param.14, f32[64,256]{1,0:T(8,128)} %param.15, f32[64,256]{1,0:T(8,128)} %param.16), kind=kLoop, calls=%fused_computation.8 | loop fusion | flops 261632 | bytes 526336 | tf_op jit(solution)/shard_map/reduce_sum | solution.py:82
  8.2 0.0 copy-start.1
  8.2 0.0 copy-start.2
  8.2 1.6 %collective-permute-start = (f32[768]{0:T(1024)S(1)}, f32[768]{0:T(1024)S(1)}, u32[]{:S(2)}, u32[]{:S(2)}) collective-permute-start(f32[768]{0:T(1024)S(1)} %slice_select_fusion), channel_id=1, source_target_pairs={{0,4},{4,0},{1,5},{5,1},{2,6},{6,2},{3,7},{7,3},{8,12},{12,8},{9,1... | collective-permute-start | bytes 9224 | tf_op jit(solution)/shard_map/ppermute | solution.py:23
  9.9 0.0 collective-permute-done.1
  9.9 0.0 collective-permute-done.2
  10.0 0.0 collective-permute-done.3
  10.0 0.1 reshape.57
  10.1 0.6 collective-permute-done
  10.7 0.1 broadcast_in_dim.27
  10.8 20.2 %all_to_all.5 = f32[32,1,832]{2,1,0:T(1,128)S(1)} all-to-all(f32[32,1,832]{2,1,0:T(1,128)S(1)} %broadcast_in_dim.27), channel_id=1, replica_groups=mesh['z'=8,'y'=4,'c'=2,'x'=4] {'z','y'}, dimensions={0} | all-to-all | bytes 212992 | tf_op jit(solution)/shard_map/all_to_all | solution.py:44
  31.0 0.1 reshape.59
  31.1 2.1 %collective-permute-start.4 = (f32[2816]{0:T(1024)S(1)}, f32[2816]{0:T(1024)S(1)}, u32[]{:S(2)}, u32[]{:S(2)}) collective-permute-start(f32[2816]{0:T(1024)S(1)} %pad_maximum_fusion.2), channel_id=1, source_target_pairs={{0,4},{4,0},{1,5},{5,1},{2,6},{6,2},{3,7},{7,3},{8,12},{12,8},{9,1... | collective-permute-start | bytes 33800 | tf_op jit(solution)/shard_map/ppermute | solution.py:23
  33.2 0.8 collective-permute-done.4
  34.1 0.0 copy-start.4
  34.1 0.0 copy-start.5
  34.2 0.1 slice.72
  34.2 0.1 slice.74
  34.4 0.7 convert_element_type.17
  35.0 0.0 copy-start.3
  35.2 0.1 pad_maximum_fusion
  35.2 59.4 %all-gather.1 = f16[4096,1536]{1,0:T(8,128)(2,1)S(1)} all-gather(f16[64,1536]{1,0:T(8,128)(2,1)S(1)} %pad_maximum_fusion), channel_id=1, replica_groups=mesh['z'=8,'y'=4,'c'=2,'x'=4] {'z','y','c'}, dimensions={0}, use_global_device_ids=true | all-gather | bytes 12779520 | tf_op jit(solution)/shard_map/all_gather | solution.py:91
  94.7 2.4 %convert_element_type.16.joined_ref = bf16[4096,1536]{1,0:T(8,128)(2,1)S(1)} convert(f16[4096,1536]{1,0:T(8,128)(2,1)S(1)} %all-gather.1) | non-fusion elementwise | flops 6291456 | bytes 25165824 | tf_op jit(solution)/shard_map/convert_element_type | solution.py:92
  97.0 0.0 copy-done
  97.0 0.0 copy-done.1
  97.1 0.0 copy-done.2
  97.1 0.0 copy-done.4
  97.1 0.0 copy-done.5
  97.1 0.0 copy-done.3
  97.1 4.7 %parted.1 = (bf16[4096,1024]{1,0:T(8,128)(2,1)}, bf16[4096,256]{1,0:T(8,128)(2,1)}, bf16[4096,256]{1,0:T(8,128)(2,1)}) custom-call(bf16[4096,1536]{1,0:T(8,128)(2,1)S(1)} %convert_element_type.16.joined_ref), custom_call_target="tpu_custom_call" | custom-call | tf_op jit(solution)/shard_map/parted/pallas_call | solution.py:66
  (25 shorter events, 0.4 us)
Async XLA Ops:
  1.3 8.6 %collective-permute-start.3 = (f32[16]{0:T(128)S(1)}, f32[16]{0:T(128)S(1)}, u32[]{:S(2)}, u32[]{:S(2)}) collective-permute-start(f32[16]{0:T(128)S(1)} %convert_convert_fusion), channel_id=1, source_target_pairs={{0,3},{1,0},{2,1},{3,2},{4,7},{5,4},{6,5},{7,6},{8,11},{9,8},{10,9... | collective-permute-start | bytes 200 | tf_op jit(solution)/shard_map/ppermute | solution.py:23
  4.6 5.3 %collective-permute-start.2 = (f32[16]{0:T(128)S(1)}, f32[16]{0:T(128)S(1)}, u32[]{:S(2)}, u32[]{:S(2)}) collective-permute-start(f32[16]{0:T(128)S(1)} %convert_convert_fusion), channel_id=1, source_target_pairs={{0,2},{1,3},{2,0},{3,1},{4,6},{5,7},{6,4},{7,5},{8,10},{9,11},{10,... | collective-permute-start | bytes 200 | tf_op jit(solution)/shard_map/ppermute | solution.py:23
  5.1 4.8 %collective-permute-start.1 = (f32[16]{0:T(128)S(1)}, f32[16]{0:T(128)S(1)}, u32[]{:S(2)}, u32[]{:S(2)}) collective-permute-start(f32[16]{0:T(128)S(1)} %convert_convert_fusion), channel_id=1, source_target_pairs={{0,1},{1,2},{2,3},{3,0},{4,5},{5,6},{6,7},{7,4},{8,9},{9,10},{10,1... | collective-permute-start | bytes 200 | tf_op jit(solution)/shard_map/ppermute | solution.py:23
  7.0 90.0 %copy-start = (f32[64,1024]{1,0:T(8,128)}, f32[64,1024]{1,0:T(8,128)S(1)}, u32[]{:S(2)}) copy-start(f32[64,1024]{1,0:T(8,128)S(1)} %get-tuple-element.21) | copy-start | bytes 786436
  8.2 88.8 %copy-start.1 = (f32[64,256]{1,0:T(8,128)}, f32[64,256]{1,0:T(8,128)S(1)}, u32[]{:S(2)}) copy-start(f32[64,256]{1,0:T(8,128)S(1)} %get-tuple-element.19) | copy-start | bytes 196612
  8.2 88.8 %copy-start.2 = (f32[64,256]{1,0:T(8,128)}, f32[64,256]{1,0:T(8,128)S(1)}, u32[]{:S(2)}) copy-start(f32[64,256]{1,0:T(8,128)S(1)} %get-tuple-element.27) | copy-start | bytes 196612
  8.2 2.4 %collective-permute-start = (f32[768]{0:T(1024)S(1)}, f32[768]{0:T(1024)S(1)}, u32[]{:S(2)}, u32[]{:S(2)}) collective-permute-start(f32[768]{0:T(1024)S(1)} %slice_select_fusion), channel_id=1, source_target_pairs={{0,4},{4,0},{1,5},{5,1},{2,6},{6,2},{3,7},{7,3},{8,12},{12,8},{9,1... | collective-permute-start | bytes 9224 | tf_op jit(solution)/shard_map/ppermute | solution.py:23
  31.1 2.9 %collective-permute-start.4 = (f32[2816]{0:T(1024)S(1)}, f32[2816]{0:T(1024)S(1)}, u32[]{:S(2)}, u32[]{:S(2)}) collective-permute-start(f32[2816]{0:T(1024)S(1)} %pad_maximum_fusion.2), channel_id=1, source_target_pairs={{0,4},{4,0},{1,5},{5,1},{2,6},{6,2},{3,7},{7,3},{8,12},{12,8},{9,1... | collective-permute-start | bytes 33800 | tf_op jit(solution)/shard_map/ppermute | solution.py:23
  34.1 63.0 %copy-start.4 = (f32[256]{0:T(256)}, f32[256]{0:T(256)S(1)}, u32[]{:S(2)}) copy-start(f32[256]{0:T(256)S(1)} %get-tuple-element.24) | copy-start | bytes 3076
  34.1 62.9 %copy-start.5 = (f32[256]{0:T(256)}, f32[256]{0:T(256)S(1)}, u32[]{:S(2)}) copy-start(f32[256]{0:T(256)S(1)} %get-tuple-element.25) | copy-start | bytes 3076
  35.0 62.0 %copy-start.3 = (f32[1024]{0:T(1024)}, f32[1024]{0:T(1024)S(1)}, u32[]{:S(2)}) copy-start(f32[1024]{0:T(1024)S(1)} %pad_maximum_fusion.3) | copy-start | bytes 12292

commit v3 on v2

--- a/solution.py
+++ b/solution.py
@@ -23,23 +23,13 @@
     return lax.ppermute(value, axis, [(i, (i + k) % n) for i in range(n)])
 
 
-def around(value, axis):
-    size = lax.axis_size(axis)
-    me = lax.axis_index(axis)
-    out = jnp.zeros((size, *value.shape), value.dtype)
-    out = lax.dynamic_update_index_in_dim(out, value, me, 0)
-    for k in range(1, size):
-        out = lax.dynamic_update_index_in_dim(out, moved(value, axis, k), (me - k) % size, 0)
-    return out
-
-
-def column_means(sums, norms, d_model):
+def column_means(sums, norm, d_model):
     c = lax.axis_index("c")
     halves = sums.reshape(2, -1)
     half = halves.shape[1]
     keep = jnp.where(c == 0, halves[0], halves[1])
     give = jnp.where(c == 0, halves[1], halves[0])
-    mine = jnp.concatenate([keep + moved(give, "c", 1), norms])
+    mine = jnp.concatenate([keep + moved(give, "c", 1), norm])
     n = lax.axis_size(("z", "y"))
     everyone = lax.all_to_all(
         jnp.broadcast_to(mine, (n, 1, mine.size)), ("z", "y"), split_axis=0, concat_axis=0, tiled=True
@@ -48,8 +38,8 @@
     other = moved(have, "c", 1)
     pair = [jnp.where(c == 0, have, other), jnp.where(c == 0, other, have)]
     means = jnp.concatenate([p[:half] for p in pair])
-    all_norms = jnp.stack([p[half:].reshape(n, -1) for p in pair], axis=1).ravel()
-    return means, all_norms
+    norms = jnp.stack([p[half:].reshape(n, -1) for p in pair], axis=1).ravel()
+    return means, norms
 
 
 def parted(joined, widths):
@@ -77,11 +67,11 @@
 def body(wq, fq, sq, wk, fk, sk, wv, fv, sv, norm_train, norm_step):
     d_model = wq.shape[0] * lax.axis_size(ROWS)
     norm = (norm_train + norm_step).astype(jnp.bfloat16)
-    norms = around(norm.astype(jnp.float32), "x").ravel()
+    xs = lax.axis_size("x")
+    slots = jnp.where(jnp.arange(xs)[:, None] == lax.axis_index("x"), norm.astype(jnp.float32)[None], 0.0).ravel()
     rq, rk, rv = step(wq, fq, sq), step(wk, fk, sk), step(wv, fv, sv)
     sums = jnp.concatenate([jnp.sum(jnp.abs(r), axis=0) for r in (rq, rk, rv)])
-    means, all_norms = column_means(sums, norms, d_model)
-    serve_norm = all_norms.astype(jnp.bfloat16)
+    means, norms = column_means(sums, slots, d_model)
     a = wq.shape[1]
     b = a + wk.shape[1]
     cq, ck, cv = means[:a], means[a:b], means[b:]
@@ -89,6 +79,10 @@
         [lax.reduce_precision(r / column, 8, 7) for r, column in ((rq, cq), (rk, ck), (rv, cv))], axis=1
     )
     whole = lax.all_gather(narrow.astype(jnp.float16), ROWS, axis=0, tiled=True)
+    norms = norms.astype(jnp.bfloat16)
+    norms = norms + moved(norms, "x", 2)
+    whole, norms = lax.optimization_barrier((whole, norms))
+    serve_norm = norms + moved(norms, "x", 1)
     final_q, final_k, final_v = parted(whole.astype(jnp.bfloat16), (a, b - a, whole.shape[1] - b))
     return final_q, final_k, final_v, cq, ck, cv, serve_norm, rq, rk, rv
 

time: 102 us -> 100 us (0.980)
  blocking collectives: 79.7 us -> 78.3 us
    all_to_all x1, blocking collectives: 20.2 us -> 18.5 us  [column_means(): lax.all_to_all(jnp.broadcast_to(mine, (n, 1, mine.size)), ('z', 'y'), spl...]
    ppermute x5 -> x4, starting transfers between devices: 8.14 us -> 8.45 us  [moved(): return lax.ppermute(value, axis, [(i, (i + k) % n) for i in range(n)])]
  transfers between devices with their start and end apart: 5 -> 4, of which waited for: 2 -> 1; matrix products, arithmetic and copies ran while one was open for 3% -> 3% of each run, Pallas kernels for 0% -> 5%
where the time goes in v3:
time: 100 us
  blocking collectives  78.3 us (78%)
  starting transfers between devices  8.45 us (8%)
  other arithmetic  6.39 us (6%)
  Pallas kernels  4.74 us (5%)
    all_gather x1, blocking collectives, body(): whole = lax.all_gather(narrow.astype(jnp.float16), ROWS, axis=0, tiled=True)  59.7 us
    all_to_all x1, blocking collectives, column_means(): lax.all_to_all(jnp.broadcast_to(mine, (n, 1, mine.size)), ('z', 'y'), spl...  18.5 us
    ppermute x4, starting transfers between devices, moved(): return lax.ppermute(value, axis, [(i, (i + k) % n) for i in range(n)])  8.45 us
    pallas_call x1, Pallas kernels, parted(): pl.pallas_call(kernel, out_shape=[jax.ShapeDtypeStruct((joined.shape[0],...  4.74 us
    reduce_sum x2, other arithmetic, body(): sums = jnp.concatenate([jnp.sum(jnp.abs(r), axis=0) for r in (rq, rk, rv)])  2.46 us
    convert_element_type x1, other arithmetic, body(): whole.astype(jnp.bfloat16)  2.35 us
  transfers between devices with their start and end apart: 4, of which 1 were waited for; matrix products, arithmetic and copies ran while one was open for 3% of the time, Pallas kernels for 5%

profile of v3, /device:TPU:1, one launch (start us, length us, event | category | flops | bytes accessed | tf_op | source)
XLA Modules:
  0.0 100.1 jit_solution(12259837598557042670)
XLA Ops:
  0.7 1.3 %abs_reduce_fusion = (f32[1024]{0:T(1024)S(1)}, f32[64,1024]{1,0:T(8,128)S(1)}) fusion(f32[64,1024]{1,0:T(8,128)} %param.11, f32[64,1024]{1,0:T(8,128)} %param.12, f32[64,1024]{1,0:T(8,128)} %param.13), kind=kLoop, calls=%fused_computation.1 | loop fusion | flops 523264 | bytes 1052672 | tf_op jit(solution)/shard_map/reduce_sum | solution.py:73
  1.9 0.0 copy-start
  1.9 1.2 %abs_reduce_fusion.1 = (f32[256]{0:T(256)S(1)}, f32[64,256]{1,0:T(8,128)S(1)}, f32[256]{0:T(256)S(1)}, f32[64,256]{1,0:T(8,128)S(1)}) fusion(f32[64,256]{1,0:T(8,128)} %param.17, f32[64,256]{1,0:T(8,128)} %param.18, f32[64,256]{1,0:T(8,128)} %param.19, f32[64,256]{1,0:T(8,128)} %param.14, f32[64,256]{1,0:T(8,128)} %param.15, f32[64,256]{1,0:T(8,128)} %param.16), kind=kLoop, calls=%fused_computation.8 | loop fusion | flops 261632 | bytes 526336 | tf_op jit(solution)/shard_map/reduce_sum | solution.py:73
  3.1 0.0 copy-start.1
  3.1 0.0 copy-start.2
  3.2 3.3 %collective-permute-start = (f32[768]{0:T(1024)S(1)}, f32[768]{0:T(1024)S(1)}, u32[]{:S(2)}, u32[]{:S(2)}) collective-permute-start(f32[768]{0:T(1024)S(1)} %slice_select_fusion), channel_id=1, source_target_pairs={{0,4},{4,0},{1,5},{5,1},{2,6},{6,2},{3,7},{7,3},{8,12},{12,8},{9,1... | collective-permute-start | bytes 9224 | tf_op jit(solution)/shard_map/ppermute | solution.py:23
  6.4 0.7 convert_convert_fusion
  7.1 0.1 broadcast_select_fusion.2
  7.2 0.1 select_n.37
  7.3 0.0 collective-permute-done
  7.3 0.1 broadcast_in_dim.31
  7.4 18.5 %all_to_all.5 = f32[32,1,832]{2,1,0:T(1,128)S(1)} all-to-all(f32[32,1,832]{2,1,0:T(1,128)S(1)} %broadcast_in_dim.31), channel_id=1, replica_groups=mesh['z'=8,'y'=4,'c'=2,'x'=4] {'z','y'}, dimensions={0} | all-to-all | bytes 212992 | tf_op jit(solution)/shard_map/all_to_all | solution.py:34
  25.9 0.1 reshape.66
  26.0 2.0 %collective-permute-start.1 = (f32[2816]{0:T(1024)S(1)}, f32[2816]{0:T(1024)S(1)}, u32[]{:S(2)}, u32[]{:S(2)}) collective-permute-start(f32[2816]{0:T(1024)S(1)} %pad_maximum_fusion.2), channel_id=1, source_target_pairs={{0,4},{4,0},{1,5},{5,1},{2,6},{6,2},{3,7},{7,3},{8,12},{12,8},{9,1... | collective-permute-start | bytes 33800 | tf_op jit(solution)/shard_map/ppermute | solution.py:23
  28.0 0.8 collective-permute-done.1
  28.9 0.0 copy-start.4
  28.9 0.0 copy-start.5
  28.9 0.1 slice.72
  29.0 0.1 slice.74
  29.1 0.1 convert_element_type.16
  29.2 2.8 %collective-permute-start.2 = (bf16[4096]{0:T(1024)(128)(2,1)S(1)}, bf16[4096]{0:T(1024)(128)(2,1)S(1)}, u32[]{:S(2)}, u32[]{:S(2)}) collective-permute-start(bf16[4096]{0:T(1024)(128)(2,1)S(1)} %convert_element_type.16), channel_id=1, source_target_pairs={{0,2},{1,3},{2,0},{3,1},{4,6},{5,7},{6,4},{7,5},{8,10},{9,11},{10,... | collective-permute-start | bytes 24584 | tf_op jit(solution)/shard_map/ppermute | solution.py:23
  32.0 0.0 copy-start.3
  32.1 0.1 pad_maximum_fusion
  32.2 59.7 %all-gather.1 = f16[4096,1536]{1,0:T(8,128)(2,1)S(1)} all-gather(f16[64,1536]{1,0:T(8,128)(2,1)S(1)} %pad_maximum_fusion), channel_id=1, replica_groups=mesh['z'=8,'y'=4,'c'=2,'x'=4] {'z','y','c'}, dimensions={0}, use_global_device_ids=true | all-gather | bytes 12779520 | tf_op jit(solution)/shard_map/all_gather | solution.py:81
  91.9 0.0 collective-permute-done.2
  91.9 0.4 collective-permute-start.3
  92.3 2.4 %convert_element_type.17.joined_ref = bf16[4096,1536]{1,0:T(8,128)(2,1)S(1)} convert(f16[4096,1536]{1,0:T(8,128)(2,1)S(1)} %all-gather.1) | non-fusion elementwise | flops 6291456 | bytes 25165824 | tf_op jit(solution)/shard_map/convert_element_type | solution.py:86
  94.7 0.0 copy-done
  94.7 0.0 copy-done.1
  94.7 0.0 copy-done.2
  94.7 0.0 copy-done.4
  94.7 0.0 copy-done.5
  94.7 0.0 copy-done.3
  94.7 4.7 %parted.1 = (bf16[4096,1024]{1,0:T(8,128)(2,1)}, bf16[4096,256]{1,0:T(8,128)(2,1)}, bf16[4096,256]{1,0:T(8,128)(2,1)}) custom-call(bf16[4096,1536]{1,0:T(8,128)(2,1)S(1)} %convert_element_type.17.joined_ref), custom_call_target="tpu_custom_call" | custom-call | tf_op jit(solution)/shard_map/parted/pallas_call | solution.py:56
  99.5 0.0 collective-permute-done.3
  99.5 0.6 add.43
  (22 shorter events, 0.2 us)
Async XLA Ops:
  1.9 92.8 %copy-start = (f32[64,1024]{1,0:T(8,128)}, f32[64,1024]{1,0:T(8,128)S(1)}, u32[]{:S(2)}) copy-start(f32[64,1024]{1,0:T(8,128)S(1)} %get-tuple-element.25) | copy-start | bytes 786436
  3.1 91.6 %copy-start.1 = (f32[64,256]{1,0:T(8,128)}, f32[64,256]{1,0:T(8,128)S(1)}, u32[]{:S(2)}) copy-start(f32[64,256]{1,0:T(8,128)S(1)} %get-tuple-element.23) | copy-start | bytes 196612
  3.1 91.6 %copy-start.2 = (f32[64,256]{1,0:T(8,128)}, f32[64,256]{1,0:T(8,128)S(1)}, u32[]{:S(2)}) copy-start(f32[64,256]{1,0:T(8,128)S(1)} %get-tuple-element.31) | copy-start | bytes 196612
  3.2 4.1 %collective-permute-start = (f32[768]{0:T(1024)S(1)}, f32[768]{0:T(1024)S(1)}, u32[]{:S(2)}, u32[]{:S(2)}) collective-permute-start(f32[768]{0:T(1024)S(1)} %slice_select_fusion), channel_id=1, source_target_pairs={{0,4},{4,0},{1,5},{5,1},{2,6},{6,2},{3,7},{7,3},{8,12},{12,8},{9,1... | collective-permute-start | bytes 9224 | tf_op jit(solution)/shard_map/ppermute | solution.py:23
  26.0 2.8 %collective-permute-start.1 = (f32[2816]{0:T(1024)S(1)}, f32[2816]{0:T(1024)S(1)}, u32[]{:S(2)}, u32[]{:S(2)}) collective-permute-start(f32[2816]{0:T(1024)S(1)} %pad_maximum_fusion.2), channel_id=1, source_target_pairs={{0,4},{4,0},{1,5},{5,1},{2,6},{6,2},{3,7},{7,3},{8,12},{12,8},{9,1... | collective-permute-start | bytes 33800 | tf_op jit(solution)/shard_map/ppermute | solution.py:23
  28.9 65.8 %copy-start.4 = (f32[256]{0:T(256)}, f32[256]{0:T(256)S(1)}, u32[]{:S(2)}) copy-start(f32[256]{0:T(256)S(1)} %get-tuple-element.28) | copy-start | bytes 3076
  28.9 65.8 %copy-start.5 = (f32[256]{0:T(256)}, f32[256]{0:T(256)S(1)}, u32[]{:S(2)}) copy-start(f32[256]{0:T(256)S(1)} %get-tuple-element.29) | copy-start | bytes 3076
  29.2 62.7 %collective-permute-start.2 = (bf16[4096]{0:T(1024)(128)(2,1)S(1)}, bf16[4096]{0:T(1024)(128)(2,1)S(1)}, u32[]{:S(2)}, u32[]{:S(2)}) collective-permute-start(bf16[4096]{0:T(1024)(128)(2,1)S(1)} %convert_element_type.16), channel_id=1, source_target_pairs={{0,2},{1,3},{2,0},{3,1},{4,6},{5,7},{6,4},{7,5},{8,10},{9,11},{10,... | collective-permute-start | bytes 24584 | tf_op jit(solution)/shard_map/ppermute | solution.py:23
  32.0 62.7 %copy-start.3 = (f32[1024]{0:T(1024)}, f32[1024]{0:T(1024)S(1)}, u32[]{:S(2)}) copy-start(f32[1024]{0:T(1024)S(1)} %pad_maximum_fusion.3) | copy-start | bytes 12292
  91.9 7.6 %collective-permute-start.3 = (bf16[4096]{0:T(1024)(128)(2,1)S(1)}, bf16[4096]{0:T(1024)(128)(2,1)S(1)}, u32[]{:S(2)}, u32[]{:S(2)}) collective-permute-start(bf16[4096]{0:T(1024)(128)(2,1)S(1)} %add.42), channel_id=1, source_target_pairs={{0,1},{1,2},{2,3},{3,0},{4,5},{5,6},{6,7},{7,4},{8,9},{9,10},{10,1... | collective-permute-start | bytes 24584 | tf_op jit(solution)/shard_map/ppermute | solution.py:23

commit v4 on v1

v4 whole, which is shorter than its diff:
```python
import jax
import jax.numpy as jnp
from jax import lax
from jax.experimental import pallas as pl
from jax.experimental.pallas import tpu as pltpu
from jax.sharding import Mesh
from jax.sharding import PartitionSpec as P

ROWS = ("z", "y", "c")
ROWS_X = ("z", "y", "c", "x")

learn_rate = 0.01
decay_rate = 0.05
tiny_value = 1e-08


def step(w, first, second):
    return w - learn_rate * (first / (jnp.sqrt(second) + tiny_value) + decay_rate * w)


def swapped(value, axis, partner):
    return lax.ppermute(value, axis, [(i, partner(i)) for i in range(lax.axis_size(axis))])


def in_order(c, mine, other):
    return [jnp.where(c == 0, mine, other), jnp.where(c == 0, other, mine)]


def parted(halves, widths):
    chips, _, rows, half = halves.shape

    def kernel(halves_ref, *refs):
        outs, sems = refs[: len(widths)], refs[len(widths) :]
        copies, column = [], 0
        for out, wide in zip(outs, widths):
            done = 0
            while done < wide:
                side, at = divmod(column, half)
                some = min(wide - done, half - at)
                copies.append(
                    pltpu.make_async_copy(
                        halves_ref.at[:, side, :, pl.ds(at, some)],
                        out.at[:, :, pl.ds(done, some)],
                        sems[len(copies)],
                    )
                )
                copies[-1].start()
                done += some
                column += some
        for copy in copies:
            copy.wait()

    return pl.pallas_call(
        kernel,
        out_shape=[jax.ShapeDtypeStruct((chips, rows, wide), halves.dtype) for wide in widths],
        in_specs=[pl.BlockSpec(memory_space=pl.ANY)],
        out_specs=[pl.BlockSpec(memory_space=pl.ANY)] * len(widths),
        scratch_shapes=[pltpu.SemaphoreType.DMA] * (len(widths) + 1),
        compiler_params=pltpu.CompilerParams(vmem_limit_bytes=1 << 20),
        name="parted",
    )(pltpu.with_memory_space_constraint(halves, pltpu.VMEM))


def body(wq, fq, sq, wk, fk, sk, wv, fv, sv, norm_train, norm_step):
    d_model = wq.shape[0] * lax.axis_size(ROWS)
    c = lax.axis_index("c")
    a, b = wq.shape[1], wk.shape[1]
    half = (a + 2 * b) // 2
    rq, rk, rv = step(wq, fq, sq), step(wk, fk, sk), step(wv, fv, sv)

    first, second = rq[:, :half], jnp.concatenate([rq[:, half:], rk, rv], axis=1)
    mine = jnp.where(c == 0, first, second)
    got = swapped(jnp.where(c == 0, second, first), "c", lambda i: 1 - i)
    sums = jnp.sum(jnp.abs(mine), axis=0) + jnp.sum(jnp.abs(got), axis=0)

    norm = (norm_train + norm_step).astype(jnp.bfloat16)
    xs = lax.axis_size("x")
    slots = jnp.where(jnp.arange(xs)[:, None] == lax.axis_index("x"), norm.astype(jnp.float32)[None], 0.0).ravel()
    have = jnp.concatenate([sums, slots])
    chips = lax.axis_size(("z", "y"))
    everyone = lax.all_to_all(
        jnp.broadcast_to(have, (chips, 1, have.size)), ("z", "y"), split_axis=0, concat_axis=0, tiled=True
    ).reshape(chips, have.size)
    mean = jnp.sum(everyone[:, :half], axis=0) / d_model
    means = jnp.concatenate(in_order(c, mean, swapped(mean, "c", lambda i: 1 - i)))
    cq, ck, cv = means[:a], means[a : a + b], means[a + b :]

    rows = jnp.concatenate(in_order(c, mine, got), axis=0)
    narrow = lax.reduce_precision(rows / mean, 8, 7).astype(jnp.float16)
    whole = lax.all_gather(narrow, ROWS, axis=0)

    norms = everyone[:, half:].astype(jnp.bfloat16)
    norms = jnp.where(jnp.arange(2)[:, None] == c, norms[:, None, :], jnp.bfloat16(0)).ravel()
    norms = norms + swapped(norms, "c", lambda i: 1 - i)
    whole, norms = lax.optimization_barrier((whole, norms))
    norms = norms + swapped(norms, "x", lambda i: i ^ 1)
    norms = norms + swapped(norms, "x", lambda i: 3 - i)

    halves = whole.astype(jnp.bfloat16).reshape(chips, 2, *narrow.shape)
    final_q, final_k, final_v = (f.reshape(d_model, -1) for f in parted(halves, (a, b, b)))
    return final_q, final_k, final_v, cq, ck, cv, norms, rq, rk, rv


def solution(mesh):
    torus = Mesh(mesh.devices.reshape(8, 4, 2, mesh.shape["model"]), ROWS_X)
    w = P(ROWS, "x")
    return jax.shard_map(
        body,
        mesh=torus,
        in_specs=(w,) * 9 + (P(ROWS_X),) * 2,
        out_specs=(P(None, "x"),) * 3 + (P("x"),) * 3 + (P(),) + (w,) * 3,
        check_vma=False,
    )
```

time: 117 us -> 103 us (0.88)
  blocking collectives: 89.8 us -> 59.5 us
  local copies, waits for them, and re-layouts: 15.8 us -> 1.49 us
  starting transfers between devices: 4.42 us -> 18.6 us
  waiting for transfers between devices: 0.49 us -> 10.2 us
  Pallas kernels: 0 us -> 4.69 us
  other arithmetic: 5.78 us -> 7.86 us
    all_to_all x1 -> x0, blocking collectives: 29.5 us -> none  [body(): lax.all_to_all(jnp.broadcast_to(mine, (n, 1, mine.size)), ROWS, split_axi...]
    all_to_all x0 -> x1, starting transfers between devices: none -> 9.5 us  [body(): lax.all_to_all(jnp.broadcast_to(have, (chips, 1, have.size)), ('z', 'y'),...]
    slice x5 -> x3, local copies, waits for them, and re-layouts: 10 us -> 0.58 us  [the longest x1 0.57 us: body(): cq, ck, cv = (means[:a], means[a:a + b], means[a + b:])]
    all_to_all x0 -> x1, waiting for transfers between devices: none -> 9.2 us  [body(): lax.all_to_all(jnp.broadcast_to(have, (chips, 1, have.size)), ('z', 'y'),...]
    pallas_call x0 -> x1, Pallas kernels: none -> 4.69 us  [parted(): pl.pallas_call(kernel, out_shape=[jax.ShapeDtypeStruct((chips, rows, wide...]
    ppermute x3 -> x5, starting transfers between devices: 4.42 us -> 9.1 us  [swapped(): lax.ppermute(value, axis, [(i, partner(i)) for i in range(lax.axis_size(a...]
    unnamed x15 -> x7, local copies, waits for them, and re-layouts: 4.61 us -> 0.03 us
    reduce_sum x3 -> x2, other arithmetic: 2.49 us -> 0.06 us  [the longest x1 0.04 us: body(): sums = jnp.sum(jnp.abs(mine), axis=0) + jnp.sum(jnp.abs(got), axis=0)]
  transfers between devices with their start and end apart: 3 -> 6, of which waited for: 1 -> 3; matrix products, arithmetic and copies ran while one was open for 2% -> 5% of each run, Pallas kernels for 0% -> 5%
where the time goes in v4:
time: 103 us
  blocking collectives  59.5 us (58%)
  starting transfers between devices  18.6 us (18%)
  waiting for transfers between devices  10.2 us (10%)
  other arithmetic  7.86 us (8%)
  Pallas kernels  4.69 us (5%)
  local copies, waits for them, and re-layouts  1.49 us (1%)
    all_gather x1, blocking collectives, body(): whole = lax.all_gather(narrow, ROWS, axis=0)  59.5 us
    all_to_all x1, starting transfers between devices, body(): lax.all_to_all(jnp.broadcast_to(have, (chips, 1, have.size)), ('z', 'y'),...  9.5 us
    all_to_all x1, waiting for transfers between devices, body(): lax.all_to_all(jnp.broadcast_to(have, (chips, 1, have.size)), ('z', 'y'),...  9.2 us
    ppermute x5, starting transfers between devices, swapped(): lax.ppermute(value, axis, [(i, partner(i)) for i in range(lax.axis_size(a...  9.1 us
    pallas_call x1, Pallas kernels, parted(): pl.pallas_call(kernel, out_shape=[jax.ShapeDtypeStruct((chips, rows, wide...  4.69 us
    convert_element_type x1, other arithmetic, body(): halves = whole.astype(jnp.bfloat16).reshape(chips, 2, *narrow.shape)  3.22 us
    sub x2, other arithmetic, step(): w - learn_rate * (first / (jnp.sqrt(second) + tiny_value) + decay_rate * w)  2.39 us
  transfers between devices with their start and end apart: 6, of which 3 were waited for; matrix products, arithmetic and copies ran while one was open for 5% of the time, Pallas kernels for 5%

profile of v4, /device:TPU:1, one launch (start us, length us, event | category | flops | bytes accessed | tf_op | source)
XLA Modules:
  0.0 103.1 jit_solution(11377325415144946626)
XLA Ops:
  0.6 1.2 %multiply_subtract_fusion = f32[64,1024]{1,0:T(8,128)S(1)} fusion(f32[64,1024]{1,0:T(8,128)} %param.11, f32[64,1024]{1,0:T(8,128)} %param.12, f32[64,1024]{1,0:T(8,128)} %param.13), kind=kLoop, calls=%fused_computation.3 | loop fusion | flops 393216 | bytes 1048576 | tf_op jit(solution)/shard_map/sub | solution.py:18
  1.9 0.0 copy-start
  1.9 1.2 %multiply_subtract_fusion.1 = (f32[64,256]{1,0:T(8,128)S(1)}, f32[64,256]{1,0:T(8,128)S(1)}) fusion(f32[64,256]{1,0:T(8,128)} %param.17, f32[64,256]{1,0:T(8,128)} %param.18, f32[64,256]{1,0:T(8,128)} %param.19, f32[64,256]{1,0:T(8,128)} %param.14, f32[64,256]{1,0:T(8,128)} %param.15, f32[64,256]{1,0:T(8,128)} %param.16), kind=kLoop, calls=%fused_computation.13 | loop fusion | flops 196608 | bytes 524288 | tf_op jit(solution)/shard_map/sub | solution.py:18
  3.1 0.0 copy-start.1
  3.1 0.0 copy-start.2
  3.1 3.3 %collective-permute-start = (f32[64,768]{1,0:T(8,128)S(1)}, f32[64,768]{1,0:T(8,128)S(1)}, u32[]{:S(2)}, u32[]{:S(2)}) collective-permute-start(f32[64,768]{1,0:T(8,128)S(1)} %get-tuple-element.23), channel_id=1, source_target_pairs={{0,4},{4,0},{1,5},{5,1},{2,6},{6,2},{3,7},{7,3},{8,12},{12,8},{9,1... | collective-permute-start | bytes 589832 | tf_op jit(solution)/shard_map/ppermute | solution.py:22
  6.4 0.7 convert_convert_fusion
  7.1 0.1 broadcast_select_fusion.3
  7.2 0.1 select_n.54
  7.3 0.2 collective-permute-done
  7.6 0.7 broadcast_in_dim.51
  8.3 9.5 %all-to-all-start = ((f32[32,1,832]{2,1,0:T(1,128)}), f32[32,1,832]{2,1,0:T(1,128)S(1)}, u32[]{:S(2)}, u32[]{:S(2)}) async-start(f32[32,1,832]{2,1,0:T(1,128)} %broadcast_in_dim.51), calls=%async_computation | async-start | bytes 229376 | tf_op jit(solution)/shard_map/all_to_all | solution.py:81
  17.8 9.2 %all-to-all-done = f32[32,1,832]{2,1,0:T(1,128)S(1)} async-done(((f32[32,1,832]{2,1,0:T(1,128)}), f32[32,1,832]{2,1,0:T(1,128)S(1)}, u32[]{:S(2)}, u32[]{:S(2)}) %all-to-all-start) | async-done | bytes 106528 | tf_op jit(solution)/shard_map/all_to_all | solution.py:81
  27.1 0.1 broadcast_select_fusion
  27.2 0.1 select_n.56
  27.3 1.9 %collective-permute-start.2 = (f32[768]{0:T(1024)S(1)}, f32[768]{0:T(1024)S(1)}, u32[]{:S(2)}, u32[]{:S(2)}) collective-permute-start(f32[768]{0:T(1024)S(1)} %broadcast_multiply_fusion), channel_id=1, source_target_pairs={{0,4},{4,0},{1,5},{5,1},{2,6},{6,2},{3,7},{7,3},{8,12},{12,8},{9,1... | collective-permute-start | bytes 9224 | tf_op jit(solution)/shard_map/ppermute | solution.py:22
  29.2 0.1 collective-permute-start.1
  29.3 0.1 fusion.1
  29.4 59.5 %all-gather.1 = f16[64,128,768]{2,1,0:T(8,128)(2,1)S(1)} all-gather(f16[1,128,768]{2,1,0:T(8,128)(2,1)S(1)} %fusion.1), channel_id=1, replica_groups=mesh['z'=8,'y'=4,'c'=2,'x'=4] {'z','y','c'}, dimensions={0}, use_global_device_ids=true | all-gather | bytes 12779520 | tf_op jit(solution)/shard_map/all_gather | solution.py:90
  88.8 0.0 collective-permute-done.2
  88.8 0.0 collective-permute-done.1
  88.9 1.3 %collective-permute-start.3 = (bf16[4096]{0:T(1024)(128)(2,1)S(1)}, bf16[4096]{0:T(1024)(128)(2,1)S(1)}, u32[]{:S(2)}, u32[]{:S(2)}) collective-permute-start(bf16[4096]{0:T(1024)(128)(2,1)S(1)} %add.45), channel_id=1, source_target_pairs={{0,1},{1,0},{2,3},{3,2},{4,5},{5,4},{6,7},{7,6},{8,9},{9,8},{10,11... | collective-permute-start | bytes 24584 | tf_op jit(solution)/shard_map/ppermute | solution.py:22
  90.2 0.6 fusion.2
  90.7 0.7 collective-permute-done.3
  91.5 2.5 %collective-permute-start.4 = (bf16[4096]{0:T(1024)(128)(2,1)S(1)}, bf16[4096]{0:T(1024)(128)(2,1)S(1)}, u32[]{:S(2)}, u32[]{:S(2)}) collective-permute-start(bf16[4096]{0:T(1024)(128)(2,1)S(1)} %add.46), channel_id=1, source_target_pairs={{0,3},{1,2},{2,1},{3,0},{4,7},{5,6},{6,5},{7,4},{8,11},{9,10},{10,... | collective-permute-start | bytes 24584 | tf_op jit(solution)/shard_map/ppermute | solution.py:22
  93.9 0.6 pad_maximum_fusion.1
  94.5 3.2 %convert_element_type.23 = bf16[64,128,768]{2,1,0:T(8,128)(2,1)S(1)} convert(f16[64,128,768]{2,1,0:T(8,128)(2,1)S(1)} %all-gather.1) | non-fusion elementwise | flops 6291456 | bytes 25165824 | tf_op jit(solution)/shard_map/convert_element_type | solution.py:99
  97.8 0.0 copy-done
  97.8 0.0 copy-done.1
  97.8 0.0 copy-done.2
  97.8 4.7 %parted.1 = (bf16[32,128,1024]{2,1,0:T(8,128)(2,1)}, bf16[32,128,256]{2,1,0:T(8,128)(2,1)}, bf16[32,128,256]{2,1,0:T(8,128)(2,1)}) custom-call(bf16[32,2,128,768]{3,2,1,0:T(8,128)(2,1)S(1)} %bitcast.11), custom_call_target="tpu_custom_call" | custom-call | tf_op jit(solution)/shard_map/parted/pallas_call | solution.py:53
  102.5 0.0 collective-permute-done.4
  102.5 0.6 add.47
  (14 shorter events, 0.2 us)
Async XLA Ops:
  1.9 95.9 %copy-start = (f32[64,1024]{1,0:T(8,128)}, f32[64,1024]{1,0:T(8,128)S(1)}, u32[]{:S(2)}) copy-start(f32[64,1024]{1,0:T(8,128)S(1)} %multiply_subtract_fusion) | copy-start | bytes 786436
  3.1 94.7 %copy-start.1 = (f32[64,256]{1,0:T(8,128)}, f32[64,256]{1,0:T(8,128)S(1)}, u32[]{:S(2)}) copy-start(f32[64,256]{1,0:T(8,128)S(1)} %get-tuple-element.29) | copy-start | bytes 196612
  3.1 94.7 %copy-start.2 = (f32[64,256]{1,0:T(8,128)}, f32[64,256]{1,0:T(8,128)S(1)}, u32[]{:S(2)}) copy-start(f32[64,256]{1,0:T(8,128)S(1)} %get-tuple-element.30) | copy-start | bytes 196612
  3.1 4.4 %collective-permute-start = (f32[64,768]{1,0:T(8,128)S(1)}, f32[64,768]{1,0:T(8,128)S(1)}, u32[]{:S(2)}, u32[]{:S(2)}) collective-permute-start(f32[64,768]{1,0:T(8,128)S(1)} %get-tuple-element.23), channel_id=1, source_target_pairs={{0,4},{4,0},{1,5},{5,1},{2,6},{6,2},{3,7},{7,3},{8,12},{12,8},{9,1... | collective-permute-start | bytes 589832 | tf_op jit(solution)/shard_map/ppermute | solution.py:22
  8.3 18.7 %all-to-all-start = ((f32[32,1,832]{2,1,0:T(1,128)}), f32[32,1,832]{2,1,0:T(1,128)S(1)}, u32[]{:S(2)}, u32[]{:S(2)}) async-start(f32[32,1,832]{2,1,0:T(1,128)} %broadcast_in_dim.51), calls=%async_computation | async-start | bytes 229376 | tf_op jit(solution)/shard_map/all_to_all | solution.py:81
  27.3 61.6 %collective-permute-start.2 = (f32[768]{0:T(1024)S(1)}, f32[768]{0:T(1024)S(1)}, u32[]{:S(2)}, u32[]{:S(2)}) collective-permute-start(f32[768]{0:T(1024)S(1)} %broadcast_multiply_fusion), channel_id=1, source_target_pairs={{0,4},{4,0},{1,5},{5,1},{2,6},{6,2},{3,7},{7,3},{8,12},{12,8},{9,1... | collective-permute-start | bytes 9224 | tf_op jit(solution)/shard_map/ppermute | solution.py:22
  29.2 59.6 %collective-permute-start.1 = (bf16[4096]{0:T(1024)(128)(2,1)S(1)}, bf16[4096]{0:T(1024)(128)(2,1)S(1)}, u32[]{:S(2)}, u32[]{:S(2)}) collective-permute-start(bf16[4096]{0:T(1024)(128)(2,1)S(1)} %select_n.56), channel_id=1, source_target_pairs={{0,4},{4,0},{1,5},{5,1},{2,6},{6,2},{3,7},{7,3},{8,12},{12,8},{9,1... | collective-permute-start | bytes 24584 | tf_op jit(solution)/shard_map/ppermute | solution.py:22
  88.9 2.6 %collective-permute-start.3 = (bf16[4096]{0:T(1024)(128)(2,1)S(1)}, bf16[4096]{0:T(1024)(128)(2,1)S(1)}, u32[]{:S(2)}, u32[]{:S(2)}) collective-permute-start(bf16[4096]{0:T(1024)(128)(2,1)S(1)} %add.45), channel_id=1, source_target_pairs={{0,1},{1,0},{2,3},{3,2},{4,5},{5,4},{6,7},{7,6},{8,9},{9,8},{10,11... | collective-permute-start | bytes 24584 | tf_op jit(solution)/shard_map/ppermute | solution.py:22
  91.5 11.0 %collective-permute-start.4 = (bf16[4096]{0:T(1024)(128)(2,1)S(1)}, bf16[4096]{0:T(1024)(128)(2,1)S(1)}, u32[]{:S(2)}, u32[]{:S(2)}) collective-permute-start(bf16[4096]{0:T(1024)(128)(2,1)S(1)} %add.46), channel_id=1, source_target_pairs={{0,3},{1,2},{2,1},{3,0},{4,7},{5,6},{6,5},{7,4},{8,11},{9,10},{10,... | collective-permute-start | bytes 24584 | tf_op jit(solution)/shard_map/ppermute | solution.py:22

commit v5 on v4

v5 whole, which is shorter than its diff:
```python
import jax
import jax.numpy as jnp
from jax import lax
from jax.experimental import pallas as pl
from jax.experimental.pallas import tpu as pltpu
from jax.sharding import Mesh
from jax.sharding import PartitionSpec as P

ROWS = ("z", "y", "c")
ROWS_X = ("z", "y", "c", "x")

learn_rate = 0.01
decay_rate = 0.05
tiny_value = 1e-08


def step(w, first, second):
    return w - learn_rate * (first / (jnp.sqrt(second) + tiny_value) + decay_rate * w)


def swapped(value, axis, partner):
    return lax.ppermute(value, axis, [(i, partner(i)) for i in range(lax.axis_size(axis))])


def in_order(c, mine, other):
    return [jnp.where(c == 0, mine, other), jnp.where(c == 0, other, mine)]


def parted(halves, means, rows, widths):
    chips, _, tall, half = halves.shape
    tile = (tall - rows, 128)

    def kernel(halves_ref, means_ref, *refs):
        outs, scales, tails, sems = refs[:3], refs[3:6], refs[6], refs[7:]
        copies, column = [], 0

        def copy(source, target):
            copies.append(pltpu.make_async_copy(source, target, sems[len(copies)]))
            copies[-1].start()

        for out, scale, wide in zip(outs, scales, widths):
            copy(means_ref.at[pl.ds(column, wide)], scale)
            done = 0
            while done < wide:
                side, at = divmod(column, half)
                some = min(wide - done, half - at)
                copy(halves_ref.at[:, side, pl.ds(0, rows), pl.ds(at, some)], out.at[:, :, pl.ds(done, some)])
                done += some
                column += some
        copy(halves_ref.at[:, :, pl.ds(rows, tile[0]), pl.ds(0, tile[1])], tails)
        for one in copies:
            one.wait()

    return pl.pallas_call(
        kernel,
        out_shape=[jax.ShapeDtypeStruct((chips, rows, wide), halves.dtype) for wide in widths]
        + [jax.ShapeDtypeStruct((wide,), means.dtype) for wide in widths]
        + [jax.ShapeDtypeStruct((chips, 2, *tile), halves.dtype)],
        in_specs=[pl.BlockSpec(memory_space=pl.ANY)] * 2,
        out_specs=[pl.BlockSpec(memory_space=pl.ANY)] * 7,
        scratch_shapes=[pltpu.SemaphoreType.DMA] * 8,
        compiler_params=pltpu.CompilerParams(vmem_limit_bytes=1 << 20),
        name="parted",
    )(*[pltpu.with_memory_space_constraint(v, pltpu.VMEM) for v in (halves, means)])


def body(wq, fq, sq, wk, fk, sk, wv, fv, sv, norm_train, norm_step):
    d_model = wq.shape[0] * lax.axis_size(ROWS)
    c = lax.axis_index("c")
    a, b = wq.shape[1], wk.shape[1]
    half = (a + 2 * b) // 2
    rq, rk, rv = step(wq, fq, sq), step(wk, fk, sk), step(wv, fv, sv)

    first, second = rq[:, :half], jnp.concatenate([rq[:, half:], rk, rv], axis=1)
    mine = jnp.where(c == 0, first, second)
    got = swapped(jnp.where(c == 0, second, first), "c", lambda i: 1 - i)
    sums = jnp.sum(jnp.abs(mine), axis=0) + jnp.sum(jnp.abs(got), axis=0)

    norm = lax.reduce_precision(norm_train + norm_step, 8, 7)
    sums, norm = lax.optimization_barrier((sums, norm))
    chips = lax.axis_size(("z", "y"))
    everyone = lax.all_to_all(
        jnp.broadcast_to(sums, (chips, 1, half)), ("z", "y"), split_axis=0, concat_axis=0, tiled=True
    ).reshape(chips, half)

    xs = lax.axis_size("x")
    slots = jnp.where(jnp.arange(xs)[:, None] == lax.axis_index("x"), norm[None], 0.0).ravel()
    slots = slots + sum(swapped(slots, "x", lambda i, k=k: (i + k) % xs) for k in range(1, xs))

    mean = jnp.sum(everyone, axis=0) / d_model
    other = swapped(mean, "c", lambda i: 1 - i)
    rows = jnp.concatenate(in_order(c, mine, got), axis=0)
    narrow = lax.reduce_precision(rows / mean, 8, 7)
    tail = jnp.broadcast_to(jnp.pad(slots, (0, half - slots.size)), (8, half))
    narrow = jnp.concatenate([narrow, tail], axis=0).astype(jnp.float16)
    whole = lax.all_gather(narrow, ROWS, axis=0)

    halves = whole.astype(jnp.bfloat16).reshape(chips, 2, *narrow.shape)
    means = jnp.concatenate(in_order(c, mean, other))
    *finals, cq, ck, cv, norms = parted(halves, means, rows.shape[0], (a, b, b))
    final_q, final_k, final_v = (f.reshape(d_model, -1) for f in finals)
    return final_q, final_k, final_v, cq, ck, cv, norms[:, :, 0, : slots.size].ravel(), rq, rk, rv


def solution(mesh):
    torus = Mesh(mesh.devices.reshape(8, 4, 2, mesh.shape["model"]), ROWS_X)
    w = P(ROWS, "x")
    return jax.shard_map(
        body,
        mesh=torus,
        in_specs=(w,) * 9 + (P(ROWS_X),) * 2,
        out_specs=(P(None, "x"),) * 3 + (P("x"),) * 3 + (P(),) + (w,) * 3,
        check_vma=False,
    )
```

time: 103 us -> 104 us (level)
  blocking collectives: 59.5 us -> 61.4 us
  other arithmetic: 7.86 us -> 6.19 us
    all_gather x1, blocking collectives: 59.5 us -> 61.4 us  [body(): whole = lax.all_gather(narrow, ROWS, axis=0)]
    all_to_all x1, starting transfers between devices: 9.5 us -> 11.2 us  [body(): lax.all_to_all(jnp.broadcast_to(sums, (chips, 1, half)), ('z', 'y'), spli...]
    ppermute x5, starting transfers between devices: 9.1 us -> 7.94 us  [swapped(): lax.ppermute(value, axis, [(i, partner(i)) for i in range(lax.axis_size(a...]
  transfers between devices with their start and end apart: 6 -> 6, of which waited for: 3 -> 2; matrix products, arithmetic and copies ran while one was open for 5% -> 4% of each run, Pallas kernels for 5% -> 0%
where the time goes in v5:
time: 104 us; the launch traced here: 103 us
  blocking collectives  61.4 us (59%)
  starting transfers between devices  19.2 us (18%)
  waiting for transfers between devices  9.43 us (9%)
  other arithmetic  6.19 us (6%)
  Pallas kernels  4.74 us (5%)
  local copies, waits for them, and re-layouts  1.6 us (2%)
    all_gather x1, blocking collectives, body(): whole = lax.all_gather(narrow, ROWS, axis=0)  61.4 us
    all_to_all x1, starting transfers between devices, body(): lax.all_to_all(jnp.broadcast_to(sums, (chips, 1, half)), ('z', 'y'), spli...  11.2 us
    all_to_all x1, waiting for transfers between devices, body(): lax.all_to_all(jnp.broadcast_to(sums, (chips, 1, half)), ('z', 'y'), spli...  9.03 us
    ppermute x5, starting transfers between devices, swapped(): lax.ppermute(value, axis, [(i, partner(i)) for i in range(lax.axis_size(a...  7.94 us
    pallas_call x1, Pallas kernels, parted(): pl.pallas_call(kernel, out_shape=[jax.ShapeDtypeStruct((chips, rows, wide...  4.74 us
    convert_element_type x1, other arithmetic, body(): halves = whole.astype(jnp.bfloat16).reshape(chips, 2, *narrow.shape)  2.73 us
    sub x2, other arithmetic, step(): w - learn_rate * (first / (jnp.sqrt(second) + tiny_value) + decay_rate * w)  2.39 us
  transfers between devices with their start and end apart: 6, of which 2 were waited for; matrix products, arithmetic and copies ran while one was open for 4% of the time, Pallas kernels for 0%

profile of v5, /device:TPU:1, one launch (start us, length us, event | category | flops | bytes accessed | tf_op | source)
XLA Modules:
  0.0 103.3 jit_solution(17392097833824470052)
XLA Ops:
  0.6 1.2 %multiply_subtract_fusion = f32[64,1024]{1,0:T(8,128)S(1)} fusion(f32[64,1024]{1,0:T(8,128)} %param.11, f32[64,1024]{1,0:T(8,128)} %param.12, f32[64,1024]{1,0:T(8,128)} %param.13), kind=kLoop, calls=%fused_computation.3 | loop fusion | flops 393216 | bytes 1048576 | tf_op jit(solution)/shard_map/sub | solution.py:18
  1.9 0.0 copy-start
  1.9 1.2 %multiply_subtract_fusion.1 = (f32[64,256]{1,0:T(8,128)S(1)}, f32[64,256]{1,0:T(8,128)S(1)}) fusion(f32[64,256]{1,0:T(8,128)} %param.17, f32[64,256]{1,0:T(8,128)} %param.18, f32[64,256]{1,0:T(8,128)} %param.19, f32[64,256]{1,0:T(8,128)} %param.14, f32[64,256]{1,0:T(8,128)} %param.15, f32[64,256]{1,0:T(8,128)} %param.16), kind=kLoop, calls=%fused_computation.13 | loop fusion | flops 196608 | bytes 524288 | tf_op jit(solution)/shard_map/sub | solution.py:18
  3.1 0.0 copy-start.1
  3.1 0.0 copy-start.2
  3.1 3.3 %collective-permute-start = (f32[64,768]{1,0:T(8,128)S(1)}, f32[64,768]{1,0:T(8,128)S(1)}, u32[]{:S(2)}, u32[]{:S(2)}) collective-permute-start(f32[64,768]{1,0:T(8,128)S(1)} %slice_select_fusion), channel_id=1, source_target_pairs={{0,4},{4,0},{1,5},{5,1},{2,6},{6,2},{3,7},{7,3},{8,12},{12,8},{9,1... | collective-permute-start | bytes 589832 | tf_op jit(solution)/shard_map/ppermute | solution.py:22
  6.4 0.7 add_reduce-precision_fusion
  7.1 0.4 collective-permute-done
  7.5 0.1 broadcast_select_fusion.1
  7.6 0.1 broadcast_select_fusion.4
  7.6 0.1 select_n.46
  7.7 0.8 collective-permute-start.3
  8.5 0.5 collective-permute-start.2
  9.0 0.6 collective-permute-start.1
  9.6 0.7 broadcast_in_dim.29
  10.3 11.2 %all-to-all-start = ((f32[32,1,768]{2,1,0:T(1,128)}), f32[32,1,768]{2,1,0:T(1,128)S(1)}, u32[]{:S(2)}, u32[]{:S(2)}) async-start(f32[32,1,768]{2,1,0:T(1,128)} %broadcast_in_dim.29), calls=%async_computation | async-start | bytes 196608 | tf_op jit(solution)/shard_map/all_to_all | solution.py:82
  21.5 0.0 collective-permute-done.3
  21.5 0.0 collective-permute-done.2
  21.6 0.0 collective-permute-done.1
  21.6 9.0 %all-to-all-done = f32[32,1,768]{2,1,0:T(1,128)S(1)} async-done(((f32[32,1,768]{2,1,0:T(1,128)}), f32[32,1,768]{2,1,0:T(1,128)S(1)}, u32[]{:S(2)}, u32[]{:S(2)}) %all-to-all-start) | async-done | bytes 98336 | tf_op jit(solution)/shard_map/all_to_all | solution.py:82
  30.6 0.1 reduce_sum.29
  30.7 2.8 %collective-permute-start.4 = (f32[768]{0:T(1024)S(1)}, f32[768]{0:T(1024)S(1)}, u32[]{:S(2)}, u32[]{:S(2)}) collective-permute-start(f32[768]{0:T(1024)S(1)} %broadcast_multiply_fusion), channel_id=1, source_target_pairs={{0,4},{4,0},{1,5},{5,1},{2,6},{6,2},{3,7},{7,3},{8,12},{12,8},{9,1... | collective-permute-start | bytes 9224 | tf_op jit(solution)/shard_map/ppermute | solution.py:22
  33.5 0.1 fusion.2
  33.5 0.1 pad_maximum_fusion
  33.6 61.4 %all-gather.1 = f16[64,136,768]{2,1,0:T(8,128)(2,1)S(1)} all-gather(f16[1,136,768]{2,1,0:T(8,128)(2,1)S(1)} %pad_maximum_fusion), channel_id=1, replica_groups=mesh['z'=8,'y'=4,'c'=2,'x'=4] {'z','y','c'}, dimensions={0}, use_global_device_ids=true | all-gather | bytes 13578240 | tf_op jit(solution)/shard_map/all_gather | solution.py:96
  95.0 0.0 copy-done
  95.0 2.7 %convert_element_type.13 = bf16[64,136,768]{2,1,0:T(8,128)(2,1)S(1)} convert(f16[64,136,768]{2,1,0:T(8,128)(2,1)S(1)} %all-gather.1) | non-fusion elementwise | flops 6684672 | bytes 26738688 | tf_op jit(solution)/shard_map/convert_element_type | solution.py:98
  97.7 0.0 copy-done.1
  97.7 0.0 copy-done.2
  97.7 0.0 collective-permute-done.4
  97.8 4.7 %parted.1 = (bf16[32,128,1024]{2,1,0:T(8,128)(2,1)}, bf16[32,128,256]{2,1,0:T(8,128)(2,1)}, bf16[32,128,256]{2,1,0:T(8,128)(2,1)}, f32[1024]{0:T(1024)}, f32[256...) custom-call(bf16[32,2,136,768]{3,2,1,0:T(8,128)(2,1)S(1)} %bitcast.6, f32[1536]{0:T(1024)S(1)} %pad_maximum_fusion.2.means_ref), custom_call_target="tpu_custom_call" | custom-call | tf_op jit(solution)/shard_map/parted/pallas_call | solution.py:54
  102.5 0.1 slice_reduce_fusion
  102.6 0.7 reshape_squeeze.3
  (10 shorter events, 0.1 us)
Async XLA Ops:
  1.9 93.1 %copy-start = (f32[64,1024]{1,0:T(8,128)}, f32[64,1024]{1,0:T(8,128)S(1)}, u32[]{:S(2)}) copy-start(f32[64,1024]{1,0:T(8,128)S(1)} %multiply_subtract_fusion) | copy-start | bytes 786436
  3.1 94.6 %copy-start.1 = (f32[64,256]{1,0:T(8,128)}, f32[64,256]{1,0:T(8,128)S(1)}, u32[]{:S(2)}) copy-start(f32[64,256]{1,0:T(8,128)S(1)} %get-tuple-element.34) | copy-start | bytes 196612
  3.1 94.6 %copy-start.2 = (f32[64,256]{1,0:T(8,128)}, f32[64,256]{1,0:T(8,128)S(1)}, u32[]{:S(2)}) copy-start(f32[64,256]{1,0:T(8,128)S(1)} %get-tuple-element.35) | copy-start | bytes 196612
  3.1 4.4 %collective-permute-start = (f32[64,768]{1,0:T(8,128)S(1)}, f32[64,768]{1,0:T(8,128)S(1)}, u32[]{:S(2)}, u32[]{:S(2)}) collective-permute-start(f32[64,768]{1,0:T(8,128)S(1)} %slice_select_fusion), channel_id=1, source_target_pairs={{0,4},{4,0},{1,5},{5,1},{2,6},{6,2},{3,7},{7,3},{8,12},{12,8},{9,1... | collective-permute-start | bytes 589832 | tf_op jit(solution)/shard_map/ppermute | solution.py:22
  7.7 13.8 %collective-permute-start.3 = (f32[64]{0:T(128)S(1)}, f32[64]{0:T(128)S(1)}, u32[]{:S(2)}, u32[]{:S(2)}) collective-permute-start(f32[64]{0:T(128)S(1)} %select_n.46), channel_id=1, source_target_pairs={{0,3},{1,0},{2,1},{3,2},{4,7},{5,4},{6,5},{7,6},{8,11},{9,8},{10,9... | collective-permute-start | bytes 776 | tf_op jit(solution)/shard_map/ppermute | solution.py:22
  8.5 13.0 %collective-permute-start.2 = (f32[64]{0:T(128)S(1)}, f32[64]{0:T(128)S(1)}, u32[]{:S(2)}, u32[]{:S(2)}) collective-permute-start(f32[64]{0:T(128)S(1)} %select_n.46), channel_id=1, source_target_pairs={{0,2},{1,3},{2,0},{3,1},{4,6},{5,7},{6,4},{7,5},{8,10},{9,11},{10,... | collective-permute-start | bytes 776 | tf_op jit(solution)/shard_map/ppermute | solution.py:22
  9.0 12.5 %collective-permute-start.1 = (f32[64]{0:T(128)S(1)}, f32[64]{0:T(128)S(1)}, u32[]{:S(2)}, u32[]{:S(2)}) collective-permute-start(f32[64]{0:T(128)S(1)} %select_n.46), channel_id=1, source_target_pairs={{0,1},{1,2},{2,3},{3,0},{4,5},{5,6},{6,7},{7,4},{8,9},{9,10},{10,1... | collective-permute-start | bytes 776 | tf_op jit(solution)/shard_map/ppermute | solution.py:22
  10.3 20.3 %all-to-all-start = ((f32[32,1,768]{2,1,0:T(1,128)}), f32[32,1,768]{2,1,0:T(1,128)S(1)}, u32[]{:S(2)}, u32[]{:S(2)}) async-start(f32[32,1,768]{2,1,0:T(1,128)} %broadcast_in_dim.29), calls=%async_computation | async-start | bytes 196608 | tf_op jit(solution)/shard_map/all_to_all | solution.py:82
  30.7 67.0 %collective-permute-start.4 = (f32[768]{0:T(1024)S(1)}, f32[768]{0:T(1024)S(1)}, u32[]{:S(2)}, u32[]{:S(2)}) collective-permute-start(f32[768]{0:T(1024)S(1)} %broadcast_multiply_fusion), channel_id=1, source_target_pairs={{0,4},{4,0},{1,5},{5,1},{2,6},{6,2},{3,7},{7,3},{8,12},{12,8},{9,1... | collective-permute-start | bytes 9224 | tf_op jit(solution)/shard_map/ppermute | solution.py:22

commit v6 on v5

v6 whole, which is shorter than its diff:
```python
import jax
import jax.numpy as jnp
from jax import lax
from jax.experimental import pallas as pl
from jax.experimental.pallas import tpu as pltpu
from jax.sharding import Mesh
from jax.sharding import PartitionSpec as P

ROWS = ("z", "y", "c")
ROWS_X = ("z", "y", "c", "x")

learn_rate = 0.01
decay_rate = 0.05
tiny_value = 1e-08


def step(w, first, second):
    return w - learn_rate * (first / (jnp.sqrt(second) + tiny_value) + decay_rate * w)


def swapped(value, axis, partner):
    return lax.ppermute(value, axis, [(i, partner(i)) for i in range(lax.axis_size(axis))])


def in_order(c, mine, other):
    return [jnp.where(c == 0, mine, other), jnp.where(c == 0, other, mine)]


def parted(halves, means, widths):
    chips, _, rows, half = halves.shape

    def kernel(halves_ref, means_ref, *refs):
        outs, scales, sems = refs[:3], refs[3:6], refs[6:]
        copies, column = [], 0

        def copy(source, target):
            copies.append(pltpu.make_async_copy(source, target, sems[len(copies)]))
            copies[-1].start()

        for out, scale, wide in zip(outs, scales, widths):
            copy(means_ref.at[pl.ds(column, wide)], scale)
            done = 0
            while done < wide:
                side, at = divmod(column, half)
                some = min(wide - done, half - at)
                copy(halves_ref.at[:, side, :, pl.ds(at, some)], out.at[:, :, pl.ds(done, some)])
                done += some
                column += some
        for one in copies:
            one.wait()

    return pl.pallas_call(
        kernel,
        out_shape=[jax.ShapeDtypeStruct((chips, rows, wide), halves.dtype) for wide in widths]
        + [jax.ShapeDtypeStruct((wide,), means.dtype) for wide in widths],
        in_specs=[pl.BlockSpec(memory_space=pl.ANY)] * 2,
        out_specs=[pl.BlockSpec(memory_space=pl.ANY)] * 6,
        scratch_shapes=[pltpu.SemaphoreType.DMA] * 7,
        compiler_params=pltpu.CompilerParams(vmem_limit_bytes=1 << 20),
        name="parted",
    )(*[pltpu.with_memory_space_constraint(v, pltpu.VMEM) for v in (halves, means)])


def body(wq, fq, sq, wk, fk, sk, wv, fv, sv, norm_train, norm_step):
    d_model = wq.shape[0] * lax.axis_size(ROWS)
    c = lax.axis_index("c")
    a, b = wq.shape[1], wk.shape[1]
    half = (a + 2 * b) // 2
    rq, rk, rv = step(wq, fq, sq), step(wk, fk, sk), step(wv, fv, sv)

    first, second = rq[:, :half], jnp.concatenate([rq[:, half:], rk, rv], axis=1)
    mine = jnp.where(c == 0, first, second)
    got = swapped(jnp.where(c == 0, second, first), "c", lambda i: 1 - i)
    sums = jnp.sum(jnp.abs(mine), axis=0) + jnp.sum(jnp.abs(got), axis=0)

    xs = lax.axis_size("x")
    mine_here = (jnp.arange(2)[:, None, None] == c) & (jnp.arange(xs)[:, None] == lax.axis_index("x"))
    slots = jnp.where(mine_here, norm_train + norm_step, 0.0).ravel()
    have = jnp.concatenate([sums, slots])
    chips = lax.axis_size(("z", "y"))
    everyone = lax.all_to_all(
        jnp.broadcast_to(have, (chips, 1, have.size)), ("z", "y"), split_axis=0, concat_axis=0, tiled=True
    ).reshape(chips, have.size)
    mean = jnp.sum(everyone[:, :half], axis=0) / d_model
    other = swapped(mean, "c", lambda i: 1 - i)
    norms = everyone[:, half:].astype(jnp.bfloat16).ravel()
    left = swapped(norms, "x", lambda i: (i + 1) % xs)
    right = swapped(norms, "x", lambda i: (i - 1) % xs)

    rows = jnp.concatenate(in_order(c, mine, got), axis=0)
    narrow = lax.reduce_precision(rows / mean, 8, 7).astype(jnp.float16)
    whole = lax.all_gather(narrow, ROWS, axis=0)

    whole, left, right = lax.optimization_barrier((whole, left, right))
    opposite = swapped(left, "x", lambda i: (i + 1) % xs)
    halves = whole.astype(jnp.bfloat16).reshape(chips, 2, *narrow.shape)
    norms = norms + left + right + opposite
    norms = norms + swapped(norms, "c", lambda i: 1 - i)
    means = jnp.concatenate(in_order(c, mean, other))
    *finals, cq, ck, cv = parted(halves, means, (a, b, b))
    final_q, final_k, final_v = (f.reshape(d_model, -1) for f in finals)
    return final_q, final_k, final_v, cq, ck, cv, norms, rq, rk, rv


def solution(mesh):
    torus = Mesh(mesh.devices.reshape(8, 4, 2, mesh.shape["model"]), ROWS_X)
    w = P(ROWS, "x")
    return jax.shard_map(
        body,
        mesh=torus,
        in_specs=(w,) * 9 + (P(ROWS_X),) * 2,
        out_specs=(P(None, "x"),) * 3 + (P("x"),) * 3 + (P(),) + (w,) * 3,
        check_vma=False,
    )
```

time: 104 us -> 104 us (level)
  blocking collectives: 61.4 us -> 77.8 us
  starting transfers between devices: 19.2 us -> 9.9 us
  waiting for transfers between devices: 9.43 us -> 3.83 us
  local copies, waits for them, and re-layouts: 1.6 us -> 0.19 us
    all_to_all x0 -> x1, blocking collectives: none -> 18.5 us  [body(): lax.all_to_all(jnp.broadcast_to(have, (chips, 1, have.size)), ('z', 'y'),...]
    all_to_all x1 -> x0, starting transfers between devices: 11.2 us -> none  [body(): lax.all_to_all(jnp.broadcast_to(sums, (chips, 1, half)), ('z', 'y'), spli...]
    all_to_all x1 -> x0, waiting for transfers between devices: 9.03 us -> none  [body(): lax.all_to_all(jnp.broadcast_to(sums, (chips, 1, half)), ('z', 'y'), spli...]
    ppermute x5 -> x6, waiting for transfers between devices: 0.4 us -> 3.83 us  [swapped(): lax.ppermute(value, axis, [(i, partner(i)) for i in range(lax.axis_size(a...]
    all_gather x1, blocking collectives: 61.4 us -> 59.3 us  [body(): whole = lax.all_gather(narrow, ROWS, axis=0)]
    ppermute x5 -> x6, starting transfers between devices: 7.94 us -> 9.9 us  [swapped(): lax.ppermute(value, axis, [(i, partner(i)) for i in range(lax.axis_size(a...]
    add x1 -> x3, other arithmetic: 0.01 us -> 1.29 us  [the longest x1 0.67 us: body(): slots = jnp.where(mine_here, norm_train + norm_step, 0.0).ravel()]
  transfers between devices with their start and end apart: 6 -> 6, of which waited for: 2 -> 2; matrix products, arithmetic and copies ran while one was open for 4% -> 4% of each run, Pallas kernels for 0% -> 5%
where the time goes in v6:
time: 104 us
  blocking collectives  77.8 us (75%)
  starting transfers between devices  9.9 us (10%)
  other arithmetic  6.92 us (7%)
  Pallas kernels  4.73 us (5%)
  waiting for transfers between devices  3.83 us (4%)
    all_gather x1, blocking collectives, body(): whole = lax.all_gather(narrow, ROWS, axis=0)  59.3 us
    all_to_all x1, blocking collectives, body(): lax.all_to_all(jnp.broadcast_to(have, (chips, 1, have.size)), ('z', 'y'),...  18.5 us
    ppermute x6, starting transfers between devices, swapped(): lax.ppermute(value, axis, [(i, partner(i)) for i in range(lax.axis_size(a...  9.9 us
    pallas_call x1, Pallas kernels, parted(): pl.pallas_call(kernel, out_shape=[jax.ShapeDtypeStruct((chips, rows, wide...  4.73 us
    ppermute x6, waiting for transfers between devices, swapped(): lax.ppermute(value, axis, [(i, partner(i)) for i in range(lax.axis_size(a...  3.83 us
    convert_element_type x1, other arithmetic, body(): halves = whole.astype(jnp.bfloat16).reshape(chips, 2, *narrow.shape)  2.89 us
    sub x2, other arithmetic, step(): w - learn_rate * (first / (jnp.sqrt(second) + tiny_value) + decay_rate * w)  2.39 us
  transfers between devices with their start and end apart: 6, of which 2 were waited for; matrix products, arithmetic and copies ran while one was open for 4% of the time, Pallas kernels for 5%

profile of v6, /device:TPU:1, one launch (start us, length us, event | category | flops | bytes accessed | tf_op | source)
XLA Modules:
  0.0 104.2 jit_solution(1072462270638025225)
XLA Ops:
  0.6 1.2 %multiply_subtract_fusion = f32[64,1024]{1,0:T(8,128)S(1)} fusion(f32[64,1024]{1,0:T(8,128)} %param.11, f32[64,1024]{1,0:T(8,128)} %param.12, f32[64,1024]{1,0:T(8,128)} %param.13), kind=kLoop, calls=%fused_computation.3 | loop fusion | flops 393216 | bytes 1048576 | tf_op jit(solution)/shard_map/sub | solution.py:18
  1.9 0.0 copy-start
  1.9 1.2 %multiply_subtract_fusion.1 = (f32[64,256]{1,0:T(8,128)S(1)}, f32[64,256]{1,0:T(8,128)S(1)}) fusion(f32[64,256]{1,0:T(8,128)} %param.17, f32[64,256]{1,0:T(8,128)} %param.18, f32[64,256]{1,0:T(8,128)} %param.19, f32[64,256]{1,0:T(8,128)} %param.14, f32[64,256]{1,0:T(8,128)} %param.15, f32[64,256]{1,0:T(8,128)} %param.16), kind=kLoop, calls=%fused_computation.13 | loop fusion | flops 196608 | bytes 524288 | tf_op jit(solution)/shard_map/sub | solution.py:18
  3.1 0.0 copy-start.1
  3.1 0.0 copy-start.2
  3.1 3.3 %collective-permute-start = (f32[64,768]{1,0:T(8,128)S(1)}, f32[64,768]{1,0:T(8,128)S(1)}, u32[]{:S(2)}, u32[]{:S(2)}) collective-permute-start(f32[64,768]{1,0:T(8,128)S(1)} %get-tuple-element.31), channel_id=1, source_target_pairs={{0,4},{4,0},{1,5},{5,1},{2,6},{6,2},{3,7},{7,3},{8,12},{12,8},{9,1... | collective-permute-start | bytes 589832 | tf_op jit(solution)/shard_map/ppermute | solution.py:22
  6.4 0.1 broadcast_and_fusion
  6.5 0.7 add.47
  7.2 0.1 broadcast_select_fusion
  7.3 0.1 select_n.46
  7.4 0.1 collective-permute-done
  7.6 0.1 broadcast_in_dim.26
  7.7 18.5 %all_to_all.5 = f32[32,1,896]{2,1,0:T(1,128)S(1)} all-to-all(f32[32,1,896]{2,1,0:T(1,128)S(1)} %broadcast_in_dim.26), channel_id=1, replica_groups=mesh['z'=8,'y'=4,'c'=2,'x'=4] {'z','y'}, dimensions={0} | all-to-all | bytes 229376 | tf_op jit(solution)/shard_map/all_to_all | solution.py:81
  26.2 1.3 %collective-permute-start.1 = (bf16[4096]{0:T(1024)(128)(2,1)S(1)}, bf16[4096]{0:T(1024)(128)(2,1)S(1)}, u32[]{:S(2)}, u32[]{:S(2)}) collective-permute-start(bf16[4096]{0:T(1024)(128)(2,1)S(1)} %fusion.2), channel_id=1, source_target_pairs={{0,1},{1,2},{2,3},{3,0},{4,5},{5,6},{6,7},{7,4},{8,9},{9,10},{10,1... | collective-permute-start | bytes 24584 | tf_op jit(solution)/shard_map/ppermute | solution.py:22
  27.5 1.5 %collective-permute-start.2 = (bf16[4096]{0:T(1024)(128)(2,1)S(1)}, bf16[4096]{0:T(1024)(128)(2,1)S(1)}, u32[]{:S(2)}, u32[]{:S(2)}) collective-permute-start(bf16[4096]{0:T(1024)(128)(2,1)S(1)} %fusion.2), channel_id=1, source_target_pairs={{0,3},{1,0},{2,1},{3,2},{4,7},{5,4},{6,5},{7,6},{8,11},{9,8},{10,9... | collective-permute-start | bytes 24584 | tf_op jit(solution)/shard_map/ppermute | solution.py:22
  29.0 2.5 %collective-permute-start.3 = (f32[768]{0:T(1024)S(1)}, f32[768]{0:T(1024)S(1)}, u32[]{:S(2)}, u32[]{:S(2)}) collective-permute-start(f32[768]{0:T(1024)S(1)} %broadcast_multiply_fusion), channel_id=1, source_target_pairs={{0,4},{4,0},{1,5},{5,1},{2,6},{6,2},{3,7},{7,3},{8,12},{12,8},{9,1... | collective-permute-start | bytes 9224 | tf_op jit(solution)/shard_map/ppermute | solution.py:22
  31.4 0.1 fusion.1
  31.5 59.3 %all-gather.1 = f16[64,128,768]{2,1,0:T(8,128)(2,1)S(1)} all-gather(f16[1,128,768]{2,1,0:T(8,128)(2,1)S(1)} %fusion.1), channel_id=1, replica_groups=mesh['z'=8,'y'=4,'c'=2,'x'=4] {'z','y','c'}, dimensions={0}, use_global_device_ids=true | all-gather | bytes 12779520 | tf_op jit(solution)/shard_map/all_gather | solution.py:92
  90.8 0.0 collective-permute-done.1
  90.8 0.0 collective-permute-done.2
  90.8 0.1 collective-permute-start.4
  90.9 0.0 collective-permute-done.3
  90.9 3.7 %collective-permute-done.4 = bf16[4096]{0:T(1024)(128)(2,1)S(1)} collective-permute-done((bf16[4096]{0:T(1024)(128)(2,1)S(1)}, bf16[4096]{0:T(1024)(128)(2,1)S(1)}, u32[]{:S(2)}, u32[]{:S(2)}) %collective-permute-start.4) | collective-permute-done | bytes 8224 | tf_op jit(solution)/shard_map/ppermute | solution.py:22
  94.6 1.3 %collective-permute-start.5 = (bf16[4096]{0:T(1024)(128)(2,1)S(1)}, bf16[4096]{0:T(1024)(128)(2,1)S(1)}, u32[]{:S(2)}, u32[]{:S(2)}) collective-permute-start(bf16[4096]{0:T(1024)(128)(2,1)S(1)} %add_add_fusion), channel_id=1, source_target_pairs={{0,4},{4,0},{1,5},{5,1},{2,6},{6,2},{3,7},{7,3},{8,12},{12,8},{9,1... | collective-permute-start | bytes 24584 | tf_op jit(solution)/shard_map/ppermute | solution.py:22
  95.9 2.9 %convert_element_type.15 = bf16[64,128,768]{2,1,0:T(8,128)(2,1)S(1)} convert(f16[64,128,768]{2,1,0:T(8,128)(2,1)S(1)} %all-gather.1) | non-fusion elementwise | flops 6291456 | bytes 25165824 | tf_op jit(solution)/shard_map/convert_element_type | solution.py:96
  98.8 0.0 copy-done
  98.8 0.0 copy-done.1
  98.8 0.0 copy-done.2
  98.8 4.7 %parted.1 = (bf16[32,128,1024]{2,1,0:T(8,128)(2,1)}, bf16[32,128,256]{2,1,0:T(8,128)(2,1)}, bf16[32,128,256]{2,1,0:T(8,128)(2,1)}, f32[1024]{0:T(1024)}, f32[256]{0:T(256)}, /*index=5*/f32[256]{0:T(256)}) custom-call(bf16[32,2,128,768]{3,2,1,0:T(8,128)(2,1)S(1)} %bitcast.15, f32[1536]{0:T(1024)S(1)} %pad_maximum_fusion.1.means_ref), custom_call_target="tpu_custom_call" | custom-call | tf_op jit(solution)/shard_map/parted/pallas_call | solution.py:52
  103.6 0.0 collective-permute-done.5
  103.6 0.6 add.51
  (14 shorter events, 0.2 us)
Async XLA Ops:
  1.9 96.9 %copy-start = (f32[64,1024]{1,0:T(8,128)}, f32[64,1024]{1,0:T(8,128)S(1)}, u32[]{:S(2)}) copy-start(f32[64,1024]{1,0:T(8,128)S(1)} %multiply_subtract_fusion) | copy-start | bytes 786436
  3.1 95.7 %copy-start.1 = (f32[64,256]{1,0:T(8,128)}, f32[64,256]{1,0:T(8,128)S(1)}, u32[]{:S(2)}) copy-start(f32[64,256]{1,0:T(8,128)S(1)} %get-tuple-element.35) | copy-start | bytes 196612
  3.1 95.7 %copy-start.2 = (f32[64,256]{1,0:T(8,128)}, f32[64,256]{1,0:T(8,128)S(1)}, u32[]{:S(2)}) copy-start(f32[64,256]{1,0:T(8,128)S(1)} %get-tuple-element.36) | copy-start | bytes 196612
  3.1 4.4 %collective-permute-start = (f32[64,768]{1,0:T(8,128)S(1)}, f32[64,768]{1,0:T(8,128)S(1)}, u32[]{:S(2)}, u32[]{:S(2)}) collective-permute-start(f32[64,768]{1,0:T(8,128)S(1)} %get-tuple-element.31), channel_id=1, source_target_pairs={{0,4},{4,0},{1,5},{5,1},{2,6},{6,2},{3,7},{7,3},{8,12},{12,8},{9,1... | collective-permute-start | bytes 589832 | tf_op jit(solution)/shard_map/ppermute | solution.py:22
  26.2 64.6 %collective-permute-start.1 = (bf16[4096]{0:T(1024)(128)(2,1)S(1)}, bf16[4096]{0:T(1024)(128)(2,1)S(1)}, u32[]{:S(2)}, u32[]{:S(2)}) collective-permute-start(bf16[4096]{0:T(1024)(128)(2,1)S(1)} %fusion.2), channel_id=1, source_target_pairs={{0,1},{1,2},{2,3},{3,0},{4,5},{5,6},{6,7},{7,4},{8,9},{9,10},{10,1... | collective-permute-start | bytes 24584 | tf_op jit(solution)/shard_map/ppermute | solution.py:22
  27.5 63.3 %collective-permute-start.2 = (bf16[4096]{0:T(1024)(128)(2,1)S(1)}, bf16[4096]{0:T(1024)(128)(2,1)S(1)}, u32[]{:S(2)}, u32[]{:S(2)}) collective-permute-start(bf16[4096]{0:T(1024)(128)(2,1)S(1)} %fusion.2), channel_id=1, source_target_pairs={{0,3},{1,0},{2,1},{3,2},{4,7},{5,4},{6,5},{7,6},{8,11},{9,8},{10,9... | collective-permute-start | bytes 24584 | tf_op jit(solution)/shard_map/ppermute | solution.py:22
  29.0 61.9 %collective-permute-start.3 = (f32[768]{0:T(1024)S(1)}, f32[768]{0:T(1024)S(1)}, u32[]{:S(2)}, u32[]{:S(2)}) collective-permute-start(f32[768]{0:T(1024)S(1)} %broadcast_multiply_fusion), channel_id=1, source_target_pairs={{0,4},{4,0},{1,5},{5,1},{2,6},{6,2},{3,7},{7,3},{8,12},{12,8},{9,1... | collective-permute-start | bytes 9224 | tf_op jit(solution)/shard_map/ppermute | solution.py:22
  90.8 3.8 %collective-permute-start.4 = (bf16[4096]{0:T(1024)(128)(2,1)S(1)}, bf16[4096]{0:T(1024)(128)(2,1)S(1)}, u32[]{:S(2)}, u32[]{:S(2)}) collective-permute-start(bf16[4096]{0:T(1024)(128)(2,1)S(1)} %collective-permute-done.1), channel_id=1, source_target_pairs={{0,1},{1,2},{2,3},{3,0},{4,5},{5,6},{6,7},{7,4},{8,9},{9,10},{10,1... | collective-permute-start | bytes 24584 | tf_op jit(solution)/shard_map/ppermute | solution.py:22
  94.6 9.0 %collective-permute-start.5 = (bf16[4096]{0:T(1024)(128)(2,1)S(1)}, bf16[4096]{0:T(1024)(128)(2,1)S(1)}, u32[]{:S(2)}, u32[]{:S(2)}) collective-permute-start(bf16[4096]{0:T(1024)(128)(2,1)S(1)} %add_add_fusion), channel_id=1, source_target_pairs={{0,4},{4,0},{1,5},{5,1},{2,6},{6,2},{3,7},{7,3},{8,12},{12,8},{9,1... | collective-permute-start | bytes 24584 | tf_op jit(solution)/shard_map/ppermute | solution.py:22

commit v7 on v6

v7 whole, which is shorter than its diff:
```python
import jax
import jax.numpy as jnp
from jax import lax
from jax.experimental import pallas as pl
from jax.experimental.pallas import tpu as pltpu
from jax.sharding import Mesh
from jax.sharding import PartitionSpec as P

ROWS = ("z", "y", "c")
ROWS_X = ("z", "y", "c", "x")

learn_rate = 0.01
decay_rate = 0.05
tiny_value = 1e-08


def step(w, first, second):
    return w - learn_rate * (first / (jnp.sqrt(second) + tiny_value) + decay_rate * w)


def swapped(value, axis, partner):
    return lax.ppermute(value, axis, [(i, partner(i)) for i in range(lax.axis_size(axis))])


def in_order(c, mine, other):
    return [jnp.where(c == 0, mine, other), jnp.where(c == 0, other, mine)]


def parted(halves, means, norms, widths):
    chips, _, rows, half = halves.shape
    half //= 2

    def kernel(halves_ref, means_ref, norms_ref, *refs):
        outs, scales, whole_norm, sems = refs[:3], refs[3:6], refs[6], refs[7:]
        copies, column = [], 0

        def copy(source, target):
            copies.append(pltpu.make_async_copy(source, target, sems[len(copies)]))
            copies[-1].start()

        for out, scale, wide in zip(outs, scales, widths):
            copy(means_ref.at[pl.ds(column, wide)], scale)
            done = 0
            while done < wide:
                side, at = divmod(column, half)
                some = min(wide - done, half - at)
                for core in range(2):
                    source = halves_ref.at[:, side, :, pl.ds(core * half + at, some)]
                    copy(source, out.at[:, core, :, pl.ds(done, some)])
                done += some
                column += some
        copy(norms_ref, whole_norm)
        for one in copies:
            one.wait()

    return pl.pallas_call(
        kernel,
        out_shape=[jax.ShapeDtypeStruct((chips, 2, rows, wide), halves.dtype) for wide in widths]
        + [jax.ShapeDtypeStruct((wide,), means.dtype) for wide in widths]
        + [jax.ShapeDtypeStruct(norms.shape, norms.dtype)],
        in_specs=[pl.BlockSpec(memory_space=pl.ANY)] * 3,
        out_specs=[pl.BlockSpec(memory_space=pl.ANY)] * 7,
        scratch_shapes=[pltpu.SemaphoreType.DMA] * 12,
        compiler_params=pltpu.CompilerParams(vmem_limit_bytes=1 << 20),
        name="parted",
    )(*[pltpu.with_memory_space_constraint(v, pltpu.VMEM) for v in (halves, means, norms)])


def body(wq, fq, sq, wk, fk, sk, wv, fv, sv, norm_train, norm_step):
    d_model = wq.shape[0] * lax.axis_size(ROWS)
    c = lax.axis_index("c")
    a, b = wq.shape[1], wk.shape[1]
    half = (a + 2 * b) // 2

    xs = lax.axis_size("x")
    mine_here = (jnp.arange(2)[:, None, None] == c) & (jnp.arange(xs)[:, None] == lax.axis_index("x"))
    slots = jnp.where(mine_here, norm_train + norm_step, 0.0).ravel()
    near = swapped(slots, "x", lambda i: i ^ 1)
    slots = slots + near
    far = swapped(slots, "x", lambda i: xs - 1 - i)
    slots = slots + far

    rq = step(wq, fq, sq)
    rk, rv = step(wk, fk, sk), step(wv, fv, sv)

    first, second = rq[:, :half], jnp.concatenate([rq[:, half:], rk, rv], axis=1)
    mine = jnp.where(c == 0, first, second)
    got = swapped(jnp.where(c == 0, second, first), "c", lambda i: 1 - i)
    sums = jnp.sum(jnp.abs(mine), axis=0) + jnp.sum(jnp.abs(got), axis=0)

    have = jnp.concatenate([sums, slots])
    chips = lax.axis_size(("z", "y"))
    everyone = lax.all_to_all(
        jnp.broadcast_to(have, (chips, 1, have.size)), ("z", "y"), split_axis=0, concat_axis=0, tiled=True
    ).reshape(chips, have.size)
    mean = jnp.sum(everyone[:, :half], axis=0) / d_model
    other = swapped(mean, "c", lambda i: 1 - i)
    norms = everyone[:, half:].astype(jnp.bfloat16).ravel()
    other_norms = swapped(norms, "c", lambda i: 1 - i)

    rows = jnp.concatenate(in_order(c, mine, got), axis=1)
    narrow = lax.reduce_precision(rows / jnp.concatenate([mean, mean]), 8, 7).astype(jnp.float16)
    whole = lax.all_gather(narrow, ROWS, axis=0)

    halves = whole.astype(jnp.bfloat16).reshape(chips, 2, *narrow.shape)
    means = jnp.concatenate(in_order(c, mean, other))
    *finals, cq, ck, cv, norms = parted(halves, means, norms + other_norms, (a, b, b))
    final_q, final_k, final_v = (f.reshape(d_model, -1) for f in finals)
    return final_q, final_k, final_v, cq, ck, cv, norms, rq, rk, rv


def solution(mesh):
    torus = Mesh(mesh.devices.reshape(8, 4, 2, mesh.shape["model"]), ROWS_X)
    w = P(ROWS, "x")
    return jax.shard_map(
        body,
        mesh=torus,
        in_specs=(w,) * 9 + (P(ROWS_X),) * 2,
        out_specs=(P(None, "x"),) * 3 + (P("x"),) * 3 + (P(),) + (w,) * 3,
        check_vma=False,
    )
```

time: 104 us -> 104 us (level)
  starting transfers between devices: 9.9 us -> 8.07 us
  waiting for transfers between devices: 3.83 us -> 5.27 us
    ppermute x6 -> x5, starting transfers between devices: 9.9 us -> 8.07 us  [swapped(): lax.ppermute(value, axis, [(i, partner(i)) for i in range(lax.axis_size(a...]
    ppermute x6 -> x5, waiting for transfers between devices: 3.83 us -> 5.27 us  [swapped(): lax.ppermute(value, axis, [(i, partner(i)) for i in range(lax.axis_size(a...]
  transfers between devices with their start and end apart: 6 -> 5, of which waited for: 2 -> 2; matrix products, arithmetic and copies ran while one was open for 4% -> 4% of each run, Pallas kernels for 5% -> 0%
where the time goes in v7:
time: 104 us
  blocking collectives  77.9 us (75%)
  starting transfers between devices  8.07 us (8%)
  other arithmetic  6.66 us (6%)
  waiting for transfers between devices  5.27 us (5%)
  Pallas kernels  4.74 us (5%)
    all_gather x1, blocking collectives, body(): whole = lax.all_gather(narrow, ROWS, axis=0)  59.4 us
    all_to_all x1, blocking collectives, body(): lax.all_to_all(jnp.broadcast_to(have, (chips, 1, have.size)), ('z', 'y'),...  18.5 us
    ppermute x5, starting transfers between devices, swapped(): lax.ppermute(value, axis, [(i, partner(i)) for i in range(lax.axis_size(a...  8.07 us
    ppermute x5, waiting for transfers between devices, swapped(): lax.ppermute(value, axis, [(i, partner(i)) for i in range(lax.axis_size(a...  5.27 us
    pallas_call x1, Pallas kernels, parted(): pl.pallas_call(kernel, out_shape=[jax.ShapeDtypeStruct((chips, 2, rows, w...  4.74 us
    convert_element_type x1, other arithmetic, body(): halves = whole.astype(jnp.bfloat16).reshape(chips, 2, *narrow.shape)  3.22 us
    sub x2, other arithmetic, step(): w - learn_rate * (first / (jnp.sqrt(second) + tiny_value) + decay_rate * w)  2.39 us
  transfers between devices with their start and end apart: 5, of which 2 were waited for; matrix products, arithmetic and copies ran while one was open for 4% of the time, Pallas kernels for 0%

profile of v7, /device:TPU:1, one launch (start us, length us, event | category | flops | bytes accessed | tf_op | source)
XLA Modules:
  0.0 103.7 jit_solution(10846221122372910283)
XLA Ops:
  0.6 1.2 %multiply_subtract_fusion = f32[64,1024]{1,0:T(8,128)S(1)} fusion(f32[64,1024]{1,0:T(8,128)} %param.11, f32[64,1024]{1,0:T(8,128)} %param.12, f32[64,1024]{1,0:T(8,128)} %param.13), kind=kLoop, calls=%fused_computation.3 | loop fusion | flops 393216 | bytes 1048576 | tf_op jit(solution)/shard_map/sub | solution.py:18
  1.9 0.0 copy-start
  1.9 1.2 %multiply_subtract_fusion.1 = (f32[64,256]{1,0:T(8,128)S(1)}, f32[64,256]{1,0:T(8,128)S(1)}) fusion(f32[64,256]{1,0:T(8,128)} %param.17, f32[64,256]{1,0:T(8,128)} %param.18, f32[64,256]{1,0:T(8,128)} %param.19, f32[64,256]{1,0:T(8,128)} %param.14, f32[64,256]{1,0:T(8,128)} %param.15, f32[64,256]{1,0:T(8,128)} %param.16), kind=kLoop, calls=%fused_computation.13 | loop fusion | flops 196608 | bytes 524288 | tf_op jit(solution)/shard_map/sub | solution.py:18
  3.1 0.0 copy-start.1
  3.1 0.0 copy-start.2
  3.1 3.3 %collective-permute-start = (f32[64,768]{1,0:T(8,128)S(1)}, f32[64,768]{1,0:T(8,128)S(1)}, u32[]{:S(2)}, u32[]{:S(2)}) collective-permute-start(f32[64,768]{1,0:T(8,128)S(1)} %get-tuple-element.27), channel_id=1, source_target_pairs={{0,4},{4,0},{1,5},{5,1},{2,6},{6,2},{3,7},{7,3},{8,12},{12,8},{9,1... | collective-permute-start | bytes 589832 | tf_op jit(solution)/shard_map/ppermute | solution.py:22
  6.5 0.1 broadcast_and_fusion
  6.5 0.7 add.44
  7.2 0.1 broadcast_select_fusion
  7.3 0.1 select_n.46
  7.4 0.0 collective-permute-start.1
  7.4 2.4 %collective-permute-done.1 = f32[128]{0:T(128)S(1)} collective-permute-done((f32[128]{0:T(128)S(1)}, f32[128]{0:T(128)S(1)}, u32[]{:S(2)}, u32[]{:S(2)}) %collective-permute-start.1) | collective-permute-done | bytes 544 | tf_op jit(solution)/shard_map/ppermute | solution.py:22
  9.8 0.8 collective-permute-start.2
  10.6 2.9 %collective-permute-done.2 = f32[128]{0:T(128)S(1)} collective-permute-done((f32[128]{0:T(128)S(1)}, f32[128]{0:T(128)S(1)}, u32[]{:S(2)}, u32[]{:S(2)}) %collective-permute-start.2) | collective-permute-done | bytes 544 | tf_op jit(solution)/shard_map/ppermute | solution.py:22
  13.4 0.0 collective-permute-done
  13.5 0.1 broadcast_in_dim.26
  13.6 18.5 %all_to_all.5 = f32[32,1,896]{2,1,0:T(1,128)S(1)} all-to-all(f32[32,1,896]{2,1,0:T(1,128)S(1)} %broadcast_in_dim.26), channel_id=1, replica_groups=mesh['z'=8,'y'=4,'c'=2,'x'=4] {'z','y'}, dimensions={0} | all-to-all | bytes 229376 | tf_op jit(solution)/shard_map/all_to_all | solution.py:93
  32.2 3.9 %collective-permute-start.3 = (f32[768]{0:T(1024)S(1)}, f32[768]{0:T(1024)S(1)}, u32[]{:S(2)}, u32[]{:S(2)}) collective-permute-start(f32[768]{0:T(1024)S(1)} %broadcast_multiply_fusion), channel_id=1, source_target_pairs={{0,4},{4,0},{1,5},{5,1},{2,6},{6,2},{3,7},{7,3},{8,12},{12,8},{9,1... | collective-permute-start | bytes 9224 | tf_op jit(solution)/shard_map/ppermute | solution.py:22
  36.1 0.1 collective-permute-start.4
  36.2 0.1 fusion.1
  36.2 59.4 %all-gather.1 = f16[64,64,1536]{2,1,0:T(8,128)(2,1)S(1)} all-gather(f16[1,64,1536]{2,1,0:T(8,128)(2,1)S(1)} %fusion.1), channel_id=1, replica_groups=mesh['z'=8,'y'=4,'c'=2,'x'=4] {'z','y','c'}, dimensions={0}, use_global_device_ids=true | all-gather | bytes 12779520 | tf_op jit(solution)/shard_map/all_gather | solution.py:103
  95.7 3.2 %convert_element_type.15 = bf16[64,64,1536]{2,1,0:T(8,128)(2,1)S(1)} convert(f16[64,64,1536]{2,1,0:T(8,128)(2,1)S(1)} %all-gather.1) | non-fusion elementwise | flops 6291456 | bytes 25165824 | tf_op jit(solution)/shard_map/convert_element_type | solution.py:105
  98.9 0.0 copy-done
  98.9 0.0 copy-done.1
  98.9 0.0 copy-done.2
  98.9 0.0 collective-permute-done.3
  99.0 0.0 collective-permute-done.4
  99.0 4.7 %parted.1 = (bf16[32,2,64,1024]{3,2,1,0:T(8,128)(2,1)}, bf16[32,2,64,256]{3,2,1,0:T(8,128)(2,1)}, bf16[32,2,64,256]{3,2,1,0:T(8,128)(2,1)}, f32[1024]{0:T(1024)}...) custom-call(bf16[32,2,64,1536]{3,2,1,0:T(8,128)(2,1)S(1)} %bitcast.15, f32[1536]{0:T(1024)S(1)} %pad_maximum_fusion.2.means_ref, ...), custom_call_target="tpu_custom_call" | custom-call | tf_op jit(solution)/shard_map/parted/pallas_call | solution.py:56
  (17 shorter events, 0.2 us)
Async XLA Ops:
  1.9 97.0 %copy-start = (f32[64,1024]{1,0:T(8,128)}, f32[64,1024]{1,0:T(8,128)S(1)}, u32[]{:S(2)}) copy-start(f32[64,1024]{1,0:T(8,128)S(1)} %multiply_subtract_fusion) | copy-start | bytes 786436
  3.1 95.8 %copy-start.1 = (f32[64,256]{1,0:T(8,128)}, f32[64,256]{1,0:T(8,128)S(1)}, u32[]{:S(2)}) copy-start(f32[64,256]{1,0:T(8,128)S(1)} %get-tuple-element.31) | copy-start | bytes 196612
  3.1 95.8 %copy-start.2 = (f32[64,256]{1,0:T(8,128)}, f32[64,256]{1,0:T(8,128)S(1)}, u32[]{:S(2)}) copy-start(f32[64,256]{1,0:T(8,128)S(1)} %get-tuple-element.32) | copy-start | bytes 196612
  3.1 10.3 %collective-permute-start = (f32[64,768]{1,0:T(8,128)S(1)}, f32[64,768]{1,0:T(8,128)S(1)}, u32[]{:S(2)}, u32[]{:S(2)}) collective-permute-start(f32[64,768]{1,0:T(8,128)S(1)} %get-tuple-element.27), channel_id=1, source_target_pairs={{0,4},{4,0},{1,5},{5,1},{2,6},{6,2},{3,7},{7,3},{8,12},{12,8},{9,1... | collective-permute-start | bytes 589832 | tf_op jit(solution)/shard_map/ppermute | solution.py:22
  7.4 2.4 %collective-permute-start.1 = (f32[128]{0:T(128)S(1)}, f32[128]{0:T(128)S(1)}, u32[]{:S(2)}, u32[]{:S(2)}) collective-permute-start(f32[128]{0:T(128)S(1)} %select_n.46), channel_id=1, source_target_pairs={{0,1},{1,0},{2,3},{3,2},{4,5},{5,4},{6,7},{7,6},{8,9},{9,8},{10,11... | collective-permute-start | bytes 1544 | tf_op jit(solution)/shard_map/ppermute | solution.py:22
  9.8 3.6 %collective-permute-start.2 = (f32[128]{0:T(128)S(1)}, f32[128]{0:T(128)S(1)}, u32[]{:S(2)}, u32[]{:S(2)}) collective-permute-start(f32[128]{0:T(128)S(1)} %add.45), channel_id=1, source_target_pairs={{0,3},{1,2},{2,1},{3,0},{4,7},{5,6},{6,5},{7,4},{8,11},{9,10},{10,... | collective-permute-start | bytes 1544 | tf_op jit(solution)/shard_map/ppermute | solution.py:22
  32.2 66.7 %collective-permute-start.3 = (f32[768]{0:T(1024)S(1)}, f32[768]{0:T(1024)S(1)}, u32[]{:S(2)}, u32[]{:S(2)}) collective-permute-start(f32[768]{0:T(1024)S(1)} %broadcast_multiply_fusion), channel_id=1, source_target_pairs={{0,4},{4,0},{1,5},{5,1},{2,6},{6,2},{3,7},{7,3},{8,12},{12,8},{9,1... | collective-permute-start | bytes 9224 | tf_op jit(solution)/shard_map/ppermute | solution.py:22
  36.1 62.9 %collective-permute-start.4 = (bf16[4096]{0:T(1024)(128)(2,1)S(1)}, bf16[4096]{0:T(1024)(128)(2,1)S(1)}, u32[]{:S(2)}, u32[]{:S(2)}) collective-permute-start(bf16[4096]{0:T(1024)(128)(2,1)S(1)} %fusion.2), channel_id=1, source_target_pairs={{0,4},{4,0},{1,5},{5,1},{2,6},{6,2},{3,7},{7,3},{8,12},{12,8},{9,1... | collective-permute-start | bytes 24584 | tf_op jit(solution)/shard_map/ppermute | solution.py:22

commit v8 on v5

--- a/solution.py
+++ b/solution.py
@@ -85,7 +85,9 @@
 
     xs = lax.axis_size("x")
     slots = jnp.where(jnp.arange(xs)[:, None] == lax.axis_index("x"), norm[None], 0.0).ravel()
-    slots = slots + sum(swapped(slots, "x", lambda i, k=k: (i + k) % xs) for k in range(1, xs))
+    opposite = swapped(slots, "x", lambda i: (i + 2) % xs)
+    slots = slots + swapped(slots, "x", lambda i: (i + 1) % xs) + swapped(slots, "x", lambda i: (i - 1) % xs)
+    slots = slots + opposite
 
     mean = jnp.sum(everyone, axis=0) / d_model
     other = swapped(mean, "c", lambda i: 1 - i)
@@ -93,7 +95,7 @@
     narrow = lax.reduce_precision(rows / mean, 8, 7)
     tail = jnp.broadcast_to(jnp.pad(slots, (0, half - slots.size)), (8, half))
     narrow = jnp.concatenate([narrow, tail], axis=0).astype(jnp.float16)
-    whole = lax.all_gather(narrow, ROWS, axis=0)
+    whole = lax.all_gather(narrow, ROWS, axis=0, tiled=True)
 
     halves = whole.astype(jnp.bfloat16).reshape(chips, 2, *narrow.shape)
     means = jnp.concatenate(in_order(c, mean, other))

time: 104 us -> 104 us (level)
  no operation moved by 1% of the time
where the time goes in v8:
time: 104 us
  blocking collectives  61.4 us (59%)
  starting transfers between devices  19.8 us (19%)
  waiting for transfers between devices  9.43 us (9%)
  other arithmetic  6.24 us (6%)
  Pallas kernels  4.74 us (5%)
  local copies, waits for them, and re-layouts  1.6 us (2%)
    all_gather x1, blocking collectives, body(): whole = lax.all_gather(narrow, ROWS, axis=0, tiled=True)  61.4 us
    all_to_all x1, starting transfers between devices, body(): lax.all_to_all(jnp.broadcast_to(sums, (chips, 1, half)), ('z', 'y'), spli...  11.2 us
    all_to_all x1, waiting for transfers between devices, body(): lax.all_to_all(jnp.broadcast_to(sums, (chips, 1, half)), ('z', 'y'), spli...  9.03 us
    ppermute x5, starting transfers between devices, swapped(): lax.ppermute(value, axis, [(i, partner(i)) for i in range(lax.axis_size(a...  8.56 us
    pallas_call x1, Pallas kernels, parted(): pl.pallas_call(kernel, out_shape=[jax.ShapeDtypeStruct((chips, rows, wide...  4.74 us
    convert_element_type x1, other arithmetic, body(): halves = whole.astype(jnp.bfloat16).reshape(chips, 2, *narrow.shape)  2.78 us
    sub x2, other arithmetic, step(): w - learn_rate * (first / (jnp.sqrt(second) + tiny_value) + decay_rate * w)  2.39 us
  transfers between devices with their start and end apart: 6, of which 2 were waited for; matrix products, arithmetic and copies ran while one was open for 4% of the time, Pallas kernels for 0%

profile of v8, /device:TPU:1, one launch (start us, length us, event | category | flops | bytes accessed | tf_op | source)
XLA Modules:
  0.0 104.0 jit_solution(10712096836370509337)
XLA Ops:
  0.6 1.2 %multiply_subtract_fusion = f32[64,1024]{1,0:T(8,128)S(1)} fusion(f32[64,1024]{1,0:T(8,128)} %param.11, f32[64,1024]{1,0:T(8,128)} %param.12, f32[64,1024]{1,0:T(8,128)} %param.13), kind=kLoop, calls=%fused_computation.3 | loop fusion | flops 393216 | bytes 1048576 | tf_op jit(solution)/shard_map/sub | solution.py:18
  1.9 0.0 copy-start
  1.9 1.2 %multiply_subtract_fusion.1 = (f32[64,256]{1,0:T(8,128)S(1)}, f32[64,256]{1,0:T(8,128)S(1)}) fusion(f32[64,256]{1,0:T(8,128)} %param.17, f32[64,256]{1,0:T(8,128)} %param.18, f32[64,256]{1,0:T(8,128)} %param.19, f32[64,256]{1,0:T(8,128)} %param.14, f32[64,256]{1,0:T(8,128)} %param.15, f32[64,256]{1,0:T(8,128)} %param.16), kind=kLoop, calls=%fused_computation.12 | loop fusion | flops 196608 | bytes 524288 | tf_op jit(solution)/shard_map/sub | solution.py:18
  3.1 0.0 copy-start.1
  3.1 0.0 copy-start.2
  3.1 3.3 %collective-permute-start = (f32[64,768]{1,0:T(8,128)S(1)}, f32[64,768]{1,0:T(8,128)S(1)}, u32[]{:S(2)}, u32[]{:S(2)}) collective-permute-start(f32[64,768]{1,0:T(8,128)S(1)} %slice_select_fusion), channel_id=1, source_target_pairs={{0,4},{4,0},{1,5},{5,1},{2,6},{6,2},{3,7},{7,3},{8,12},{12,8},{9,1... | collective-permute-start | bytes 589832 | tf_op jit(solution)/shard_map/ppermute | solution.py:22
  6.4 0.7 add_reduce-precision_fusion
  7.1 0.4 collective-permute-done
  7.5 0.1 broadcast_select_fusion.1
  7.6 0.1 broadcast_select_fusion.4
  7.6 0.1 select_n.46
  7.7 1.0 %collective-permute-start.3 = (f32[64]{0:T(128)S(1)}, f32[64]{0:T(128)S(1)}, u32[]{:S(2)}, u32[]{:S(2)}) collective-permute-start(f32[64]{0:T(128)S(1)} %select_n.46), channel_id=1, source_target_pairs={{0,2},{1,3},{2,0},{3,1},{4,6},{5,7},{6,4},{7,5},{8,10},{9,11},{10,... | collective-permute-start | bytes 776 | tf_op jit(solution)/shard_map/ppermute | solution.py:22
  8.8 0.9 collective-permute-start.2
  9.6 0.6 collective-permute-start.1
  10.2 0.7 broadcast_in_dim.29
  10.9 11.2 %all-to-all-start = ((f32[32,1,768]{2,1,0:T(1,128)}), f32[32,1,768]{2,1,0:T(1,128)S(1)}, u32[]{:S(2)}, u32[]{:S(2)}) async-start(f32[32,1,768]{2,1,0:T(1,128)} %broadcast_in_dim.29), calls=%async_computation | async-start | bytes 196608 | tf_op jit(solution)/shard_map/all_to_all | solution.py:82
  22.2 0.0 collective-permute-done.3
  22.2 0.0 collective-permute-done.2
  22.2 0.0 collective-permute-done.1
  22.2 9.0 %all-to-all-done = f32[32,1,768]{2,1,0:T(1,128)S(1)} async-done(((f32[32,1,768]{2,1,0:T(1,128)}), f32[32,1,768]{2,1,0:T(1,128)S(1)}, u32[]{:S(2)}, u32[]{:S(2)}) %all-to-all-start) | async-done | bytes 98336 | tf_op jit(solution)/shard_map/all_to_all | solution.py:82
  31.2 0.1 reduce_sum.29
  31.3 2.8 %collective-permute-start.4 = (f32[768]{0:T(1024)S(1)}, f32[768]{0:T(1024)S(1)}, u32[]{:S(2)}, u32[]{:S(2)}) collective-permute-start(f32[768]{0:T(1024)S(1)} %broadcast_multiply_fusion), channel_id=1, source_target_pairs={{0,4},{4,0},{1,5},{5,1},{2,6},{6,2},{3,7},{7,3},{8,12},{12,8},{9,1... | collective-permute-start | bytes 9224 | tf_op jit(solution)/shard_map/ppermute | solution.py:22
  34.1 0.1 fusion.1
  34.2 0.1 pad_maximum_fusion
  34.2 61.4 %all-gather.1 = f16[8704,768]{1,0:T(8,128)(2,1)S(1)} all-gather(f16[136,768]{1,0:T(8,128)(2,1)S(1)} %pad_maximum_fusion), channel_id=1, replica_groups=mesh['z'=8,'y'=4,'c'=2,'x'=4] {'z','y','c'}, dimensions={0}, use_global_device_ids=true | all-gather | bytes 13578240 | tf_op jit(solution)/shard_map/all_gather | solution.py:98
  95.6 0.0 copy-done
  95.6 2.8 %convert_element_type.6 = bf16[8704,768]{1,0:T(8,128)(2,1)S(1)} convert(f16[8704,768]{1,0:T(8,128)(2,1)S(1)} %all-gather.1) | non-fusion elementwise | flops 6684672 | bytes 26738688 | tf_op jit(solution)/shard_map/convert_element_type | solution.py:100
  98.4 0.0 copy-done.1
  98.4 0.0 copy-done.2
  98.4 0.0 collective-permute-done.4
  98.4 4.7 %parted.1 = (bf16[32,128,1024]{2,1,0:T(8,128)(2,1)}, bf16[32,128,256]{2,1,0:T(8,128)(2,1)}, bf16[32,128,256]{2,1,0:T(8,128)(2,1)}, f32[1024]{0:T(1024)}, f32[256...) custom-call(bf16[32,2,136,768]{3,2,1,0:T(8,128)(2,1)S(1)} %bitcast.4, f32[1536]{0:T(1024)S(1)} %pad_maximum_fusion.2.means_ref), custom_call_target="tpu_custom_call" | custom-call | tf_op jit(solution)/shard_map/parted/pallas_call | solution.py:54
  103.2 0.1 slice_reduce_fusion
  103.3 0.7 reshape_squeeze.3
  (10 shorter events, 0.1 us)
Async XLA Ops:
  1.9 93.7 %copy-start = (f32[64,1024]{1,0:T(8,128)}, f32[64,1024]{1,0:T(8,128)S(1)}, u32[]{:S(2)}) copy-start(f32[64,1024]{1,0:T(8,128)S(1)} %multiply_subtract_fusion) | copy-start | bytes 786436
  3.1 95.3 %copy-start.1 = (f32[64,256]{1,0:T(8,128)}, f32[64,256]{1,0:T(8,128)S(1)}, u32[]{:S(2)}) copy-start(f32[64,256]{1,0:T(8,128)S(1)} %get-tuple-element.34) | copy-start | bytes 196612
  3.1 95.3 %copy-start.2 = (f32[64,256]{1,0:T(8,128)}, f32[64,256]{1,0:T(8,128)S(1)}, u32[]{:S(2)}) copy-start(f32[64,256]{1,0:T(8,128)S(1)} %get-tuple-element.35) | copy-start | bytes 196612
  3.1 4.4 %collective-permute-start = (f32[64,768]{1,0:T(8,128)S(1)}, f32[64,768]{1,0:T(8,128)S(1)}, u32[]{:S(2)}, u32[]{:S(2)}) collective-permute-start(f32[64,768]{1,0:T(8,128)S(1)} %slice_select_fusion), channel_id=1, source_target_pairs={{0,4},{4,0},{1,5},{5,1},{2,6},{6,2},{3,7},{7,3},{8,12},{12,8},{9,1... | collective-permute-start | bytes 589832 | tf_op jit(solution)/shard_map/ppermute | solution.py:22
  7.7 14.4 %collective-permute-start.3 = (f32[64]{0:T(128)S(1)}, f32[64]{0:T(128)S(1)}, u32[]{:S(2)}, u32[]{:S(2)}) collective-permute-start(f32[64]{0:T(128)S(1)} %select_n.46), channel_id=1, source_target_pairs={{0,2},{1,3},{2,0},{3,1},{4,6},{5,7},{6,4},{7,5},{8,10},{9,11},{10,... | collective-permute-start | bytes 776 | tf_op jit(solution)/shard_map/ppermute | solution.py:22
  8.8 13.4 %collective-permute-start.2 = (f32[64]{0:T(128)S(1)}, f32[64]{0:T(128)S(1)}, u32[]{:S(2)}, u32[]{:S(2)}) collective-permute-start(f32[64]{0:T(128)S(1)} %select_n.46), channel_id=1, source_target_pairs={{0,3},{1,0},{2,1},{3,2},{4,7},{5,4},{6,5},{7,6},{8,11},{9,8},{10,9... | collective-permute-start | bytes 776 | tf_op jit(solution)/shard_map/ppermute | solution.py:22
  9.6 12.5 %collective-permute-start.1 = (f32[64]{0:T(128)S(1)}, f32[64]{0:T(128)S(1)}, u32[]{:S(2)}, u32[]{:S(2)}) collective-permute-start(f32[64]{0:T(128)S(1)} %select_n.46), channel_id=1, source_target_pairs={{0,1},{1,2},{2,3},{3,0},{4,5},{5,6},{6,7},{7,4},{8,9},{9,10},{10,1... | collective-permute-start | bytes 776 | tf_op jit(solution)/shard_map/ppermute | solution.py:22
  10.9 20.3 %all-to-all-start = ((f32[32,1,768]{2,1,0:T(1,128)}), f32[32,1,768]{2,1,0:T(1,128)S(1)}, u32[]{:S(2)}, u32[]{:S(2)}) async-start(f32[32,1,768]{2,1,0:T(1,128)} %broadcast_in_dim.29), calls=%async_computation | async-start | bytes 196608 | tf_op jit(solution)/shard_map/all_to_all | solution.py:82
  31.3 67.1 %collective-permute-start.4 = (f32[768]{0:T(1024)S(1)}, f32[768]{0:T(1024)S(1)}, u32[]{:S(2)}, u32[]{:S(2)}) collective-permute-start(f32[768]{0:T(1024)S(1)} %broadcast_multiply_fusion), channel_id=1, source_target_pairs={{0,4},{4,0},{1,5},{5,1},{2,6},{6,2},{3,7},{7,3},{8,12},{12,8},{9,1... | collective-permute-start | bytes 9224 | tf_op jit(solution)/shard_map/ppermute | solution.py:22

commit v9 on v3

--- a/solution.py
+++ b/solution.py
@@ -34,12 +34,10 @@
     everyone = lax.all_to_all(
         jnp.broadcast_to(mine, (n, 1, mine.size)), ("z", "y"), split_axis=0, concat_axis=0, tiled=True
     ).reshape(n, mine.size)
-    have = jnp.concatenate([jnp.sum(everyone[:, :half], axis=0) / d_model, everyone[:, half:].ravel()])
+    have = jnp.sum(everyone[:, :half], axis=0) / d_model
     other = moved(have, "c", 1)
-    pair = [jnp.where(c == 0, have, other), jnp.where(c == 0, other, have)]
-    means = jnp.concatenate([p[:half] for p in pair])
-    norms = jnp.stack([p[half:].reshape(n, -1) for p in pair], axis=1).ravel()
-    return means, norms
+    means = jnp.concatenate([jnp.where(c == 0, have, other), jnp.where(c == 0, other, have)])
+    return means, everyone[:, half:].astype(jnp.bfloat16).ravel()
 
 
 def parted(joined, widths):
@@ -66,9 +64,9 @@
 
 def body(wq, fq, sq, wk, fk, sk, wv, fv, sv, norm_train, norm_step):
     d_model = wq.shape[0] * lax.axis_size(ROWS)
-    norm = (norm_train + norm_step).astype(jnp.bfloat16)
-    xs = lax.axis_size("x")
-    slots = jnp.where(jnp.arange(xs)[:, None] == lax.axis_index("x"), norm.astype(jnp.float32)[None], 0.0).ravel()
+    c, x = lax.axis_index("c"), lax.axis_index("x")
+    mine_here = (jnp.arange(2)[:, None, None] == c) & (jnp.arange(lax.axis_size("x"))[:, None] == x)
+    slots = jnp.where(mine_here, norm_train + norm_step, 0.0).ravel()
     rq, rk, rv = step(wq, fq, sq), step(wk, fk, sk), step(wv, fv, sv)
     sums = jnp.concatenate([jnp.sum(jnp.abs(r), axis=0) for r in (rq, rk, rv)])
     means, norms = column_means(sums, slots, d_model)
@@ -79,11 +77,14 @@
         [lax.reduce_precision(r / column, 8, 7) for r, column in ((rq, cq), (rk, ck), (rv, cv))], axis=1
     )
     whole = lax.all_gather(narrow.astype(jnp.float16), ROWS, axis=0, tiled=True)
-    norms = norms.astype(jnp.bfloat16)
-    norms = norms + moved(norms, "x", 2)
-    whole, norms = lax.optimization_barrier((whole, norms))
+    opposite = moved(norms, "x", 2)
+    whole, opposite = lax.optimization_barrier((whole, opposite))
+    norms = norms + opposite
+    partner = moved(norms, "c", 1)
+    norms = norms + partner
+    joined = whole.astype(jnp.bfloat16)
     serve_norm = norms + moved(norms, "x", 1)
-    final_q, final_k, final_v = parted(whole.astype(jnp.bfloat16), (a, b - a, whole.shape[1] - b))
+    final_q, final_k, final_v = parted(joined, (a, b - a, whole.shape[1] - b))
     return final_q, final_k, final_v, cq, ck, cv, serve_norm, rq, rk, rv
 
 

time: 100 us -> 100 us (level)
    convert_element_type x2 -> x1, other arithmetic: 3.03 us -> 2.35 us  [body(): joined = whole.astype(jnp.bfloat16)]
    ppermute x4 -> x5, starting transfers between devices: 8.45 us -> 8.49 us  [moved(): return lax.ppermute(value, axis, [(i, (i + k) % n) for i in range(n)])]
  transfers between devices with their start and end apart: 4 -> 5, of which waited for: 1 -> 1; matrix products, arithmetic and copies ran while one was open for 3% -> 3% of each run, Pallas kernels for 5% -> 5%
where the time goes in v9:
time: 100 us
  blocking collectives  78.1 us (78%)
  starting transfers between devices  8.49 us (8%)
  other arithmetic  6.46 us (6%)
  Pallas kernels  4.74 us (5%)
  waiting for transfers between devices  1.12 us (1%)
    all_gather x1, blocking collectives, body(): whole = lax.all_gather(narrow.astype(jnp.float16), ROWS, axis=0, tiled=True)  59.6 us
    all_to_all x1, blocking collectives, column_means(): lax.all_to_all(jnp.broadcast_to(mine, (n, 1, mine.size)), ('z', 'y'), spl...  18.5 us
    ppermute x5, starting transfers between devices, moved(): return lax.ppermute(value, axis, [(i, (i + k) % n) for i in range(n)])  8.49 us
    pallas_call x1, Pallas kernels, parted(): pl.pallas_call(kernel, out_shape=[jax.ShapeDtypeStruct((joined.shape[0],...  4.74 us
    reduce_sum x2, other arithmetic, body(): sums = jnp.concatenate([jnp.sum(jnp.abs(r), axis=0) for r in (rq, rk, rv)])  2.46 us
    convert_element_type x1, other arithmetic, body(): joined = whole.astype(jnp.bfloat16)  2.35 us
  transfers between devices with their start and end apart: 5, of which 1 were waited for; matrix products, arithmetic and copies ran while one was open for 3% of the time, Pallas kernels for 5%

profile of v9, /device:TPU:1, one launch (start us, length us, event | category | flops | bytes accessed | tf_op | source)
XLA Modules:
  0.0 100.0 jit_solution(9052580142752278337)
XLA Ops:
  0.7 1.3 %abs_reduce_fusion = (f32[1024]{0:T(1024)S(1)}, f32[64,1024]{1,0:T(8,128)S(1)}) fusion(f32[64,1024]{1,0:T(8,128)} %param.11, f32[64,1024]{1,0:T(8,128)} %param.12, f32[64,1024]{1,0:T(8,128)} %param.13), kind=kLoop, calls=%fused_computation.1 | loop fusion | flops 523264 | bytes 1052672 | tf_op jit(solution)/shard_map/reduce_sum | solution.py:71
  1.9 0.0 copy-start
  1.9 1.2 %abs_reduce_fusion.1 = (f32[256]{0:T(256)S(1)}, f32[64,256]{1,0:T(8,128)S(1)}, f32[256]{0:T(256)S(1)}, f32[64,256]{1,0:T(8,128)S(1)}) fusion(f32[64,256]{1,0:T(8,128)} %param.17, f32[64,256]{1,0:T(8,128)} %param.18, f32[64,256]{1,0:T(8,128)} %param.19, f32[64,256]{1,0:T(8,128)} %param.14, f32[64,256]{1,0:T(8,128)} %param.15, f32[64,256]{1,0:T(8,128)} %param.16), kind=kLoop, calls=%fused_computation.8 | loop fusion | flops 261632 | bytes 526336 | tf_op jit(solution)/shard_map/reduce_sum | solution.py:71
  3.1 0.0 copy-start.1
  3.1 0.0 copy-start.2
  3.2 3.3 %collective-permute-start = (f32[768]{0:T(1024)S(1)}, f32[768]{0:T(1024)S(1)}, u32[]{:S(2)}, u32[]{:S(2)}) collective-permute-start(f32[768]{0:T(1024)S(1)} %slice_select_fusion), channel_id=1, source_target_pairs={{0,4},{4,0},{1,5},{5,1},{2,6},{6,2},{3,7},{7,3},{8,12},{12,8},{9,1... | collective-permute-start | bytes 9224 | tf_op jit(solution)/shard_map/ppermute | solution.py:23
  6.5 0.1 broadcast_and_fusion
  6.5 0.7 add.44
  7.2 0.1 broadcast_select_fusion
  7.3 0.1 select_n.32
  7.4 0.0 collective-permute-done
  7.4 0.1 broadcast_in_dim.28
  7.5 18.5 %all_to_all.5 = f32[32,1,896]{2,1,0:T(1,128)S(1)} all-to-all(f32[32,1,896]{2,1,0:T(1,128)S(1)} %broadcast_in_dim.28), channel_id=1, replica_groups=mesh['z'=8,'y'=4,'c'=2,'x'=4] {'z','y'}, dimensions={0} | all-to-all | bytes 229376 | tf_op jit(solution)/shard_map/all_to_all | solution.py:34
  26.0 2.0 %collective-permute-start.1 = (f32[768]{0:T(1024)S(1)}, f32[768]{0:T(1024)S(1)}, u32[]{:S(2)}, u32[]{:S(2)}) collective-permute-start(f32[768]{0:T(1024)S(1)} %broadcast_multiply_fusion), channel_id=1, source_target_pairs={{0,4},{4,0},{1,5},{5,1},{2,6},{6,2},{3,7},{7,3},{8,12},{12,8},{9,1... | collective-permute-start | bytes 9224 | tf_op jit(solution)/shard_map/ppermute | solution.py:23
  28.0 2.7 %collective-permute-start.2 = (bf16[4096]{0:T(1024)(128)(2,1)S(1)}, bf16[4096]{0:T(1024)(128)(2,1)S(1)}, u32[]{:S(2)}, u32[]{:S(2)}) collective-permute-start(bf16[4096]{0:T(1024)(128)(2,1)S(1)} %fusion), channel_id=1, source_target_pairs={{0,2},{1,3},{2,0},{3,1},{4,6},{5,7},{6,4},{7,5},{8,10},{9,11},{10,... | collective-permute-start | bytes 24584 | tf_op jit(solution)/shard_map/ppermute | solution.py:23
  30.8 0.0 collective-permute-done.1
  30.8 0.0 copy-start.4
  30.8 0.0 copy-start.5
  30.8 0.0 copy-start.3
  31.0 0.1 pad_maximum_fusion
  31.0 59.6 %all-gather.1 = f16[4096,1536]{1,0:T(8,128)(2,1)S(1)} all-gather(f16[64,1536]{1,0:T(8,128)(2,1)S(1)} %pad_maximum_fusion), channel_id=1, replica_groups=mesh['z'=8,'y'=4,'c'=2,'x'=4] {'z','y','c'}, dimensions={0}, use_global_device_ids=true | all-gather | bytes 12779520 | tf_op jit(solution)/shard_map/all_gather | solution.py:79
  90.6 0.0 collective-permute-done.2
  90.6 0.1 collective-permute-start.3
  90.8 1.1 %collective-permute-done.3 = bf16[4096]{0:T(1024)(128)(2,1)S(1)} collective-permute-done((bf16[4096]{0:T(1024)(128)(2,1)S(1)}, bf16[4096]{0:T(1024)(128)(2,1)S(1)}, u32[]{:S(2)}, u32[]{:S(2)}) %collective-permute-start.3) | collective-permute-done | bytes 8224 | tf_op jit(solution)/shard_map/ppermute | solution.py:23
  91.9 0.3 collective-permute-start.4
  92.2 2.4 %convert_element_type.2.joined_ref = bf16[4096,1536]{1,0:T(8,128)(2,1)S(1)} convert(f16[4096,1536]{1,0:T(8,128)(2,1)S(1)} %all-gather.1) | non-fusion elementwise | flops 6291456 | bytes 25165824 | tf_op jit(solution)/shard_map/convert_element_type | solution.py:85
  94.6 0.0 copy-done
  94.6 0.0 copy-done.1
  94.6 0.0 copy-done.2
  94.6 0.0 copy-done.4
  94.6 0.0 copy-done.5
  94.6 0.0 copy-done.3
  94.6 4.7 %parted.1 = (bf16[4096,1024]{1,0:T(8,128)(2,1)}, bf16[4096,256]{1,0:T(8,128)(2,1)}, bf16[4096,256]{1,0:T(8,128)(2,1)}) custom-call(bf16[4096,1536]{1,0:T(8,128)(2,1)S(1)} %convert_element_type.2.joined_ref), custom_call_target="tpu_custom_call" | custom-call | tf_op jit(solution)/shard_map/parted/pallas_call | solution.py:54
  99.4 0.0 collective-permute-done.4
  99.4 0.6 add.47
  (17 shorter events, 0.2 us)
Async XLA Ops:
  1.9 92.7 %copy-start = (f32[64,1024]{1,0:T(8,128)}, f32[64,1024]{1,0:T(8,128)S(1)}, u32[]{:S(2)}) copy-start(f32[64,1024]{1,0:T(8,128)S(1)} %get-tuple-element.25) | copy-start | bytes 786436
  3.1 91.5 %copy-start.1 = (f32[64,256]{1,0:T(8,128)}, f32[64,256]{1,0:T(8,128)S(1)}, u32[]{:S(2)}) copy-start(f32[64,256]{1,0:T(8,128)S(1)} %get-tuple-element.23) | copy-start | bytes 196612
  3.1 91.5 %copy-start.2 = (f32[64,256]{1,0:T(8,128)}, f32[64,256]{1,0:T(8,128)S(1)}, u32[]{:S(2)}) copy-start(f32[64,256]{1,0:T(8,128)S(1)} %get-tuple-element.31) | copy-start | bytes 196612
  3.2 4.2 %collective-permute-start = (f32[768]{0:T(1024)S(1)}, f32[768]{0:T(1024)S(1)}, u32[]{:S(2)}, u32[]{:S(2)}) collective-permute-start(f32[768]{0:T(1024)S(1)} %slice_select_fusion), channel_id=1, source_target_pairs={{0,4},{4,0},{1,5},{5,1},{2,6},{6,2},{3,7},{7,3},{8,12},{12,8},{9,1... | collective-permute-start | bytes 9224 | tf_op jit(solution)/shard_map/ppermute | solution.py:23
  26.0 4.8 %collective-permute-start.1 = (f32[768]{0:T(1024)S(1)}, f32[768]{0:T(1024)S(1)}, u32[]{:S(2)}, u32[]{:S(2)}) collective-permute-start(f32[768]{0:T(1024)S(1)} %broadcast_multiply_fusion), channel_id=1, source_target_pairs={{0,4},{4,0},{1,5},{5,1},{2,6},{6,2},{3,7},{7,3},{8,12},{12,8},{9,1... | collective-permute-start | bytes 9224 | tf_op jit(solution)/shard_map/ppermute | solution.py:23
  28.0 62.6 %collective-permute-start.2 = (bf16[4096]{0:T(1024)(128)(2,1)S(1)}, bf16[4096]{0:T(1024)(128)(2,1)S(1)}, u32[]{:S(2)}, u32[]{:S(2)}) collective-permute-start(bf16[4096]{0:T(1024)(128)(2,1)S(1)} %fusion), channel_id=1, source_target_pairs={{0,2},{1,3},{2,0},{3,1},{4,6},{5,7},{6,4},{7,5},{8,10},{9,11},{10,... | collective-permute-start | bytes 24584 | tf_op jit(solution)/shard_map/ppermute | solution.py:23
  30.8 63.8 %copy-start.4 = (f32[256]{0:T(256)}, f32[256]{0:T(256)S(1)}, u32[]{:S(2)}) copy-start(f32[256]{0:T(256)S(1)} %get-tuple-element.28) | copy-start | bytes 3076
  30.8 63.8 %copy-start.5 = (f32[256]{0:T(256)}, f32[256]{0:T(256)S(1)}, u32[]{:S(2)}) copy-start(f32[256]{0:T(256)S(1)} %get-tuple-element.29) | copy-start | bytes 3076
  30.8 63.8 %copy-start.3 = (f32[1024]{0:T(1024)}, f32[1024]{0:T(1024)S(1)}, u32[]{:S(2)}) copy-start(f32[1024]{0:T(1024)S(1)} %pad_maximum_fusion.1) | copy-start | bytes 12292
  90.6 1.3 %collective-permute-start.3 = (bf16[4096]{0:T(1024)(128)(2,1)S(1)}, bf16[4096]{0:T(1024)(128)(2,1)S(1)}, u32[]{:S(2)}, u32[]{:S(2)}) collective-permute-start(bf16[4096]{0:T(1024)(128)(2,1)S(1)} %fusion.2), channel_id=1, source_target_pairs={{0,4},{4,0},{1,5},{5,1},{2,6},{6,2},{3,7},{7,3},{8,12},{12,8},{9,1... | collective-permute-start | bytes 24584 | tf_op jit(solution)/shard_map/ppermute | solution.py:23
  91.9 7.5 %collective-permute-start.4 = (bf16[4096]{0:T(1024)(128)(2,1)S(1)}, bf16[4096]{0:T(1024)(128)(2,1)S(1)}, u32[]{:S(2)}, u32[]{:S(2)}) collective-permute-start(bf16[4096]{0:T(1024)(128)(2,1)S(1)} %add.46), channel_id=1, source_target_pairs={{0,1},{1,2},{2,3},{3,0},{4,5},{5,6},{6,7},{7,4},{8,9},{9,10},{10,1... | collective-permute-start | bytes 24584 | tf_op jit(solution)/shard_map/ppermute | solution.py:23
